TPU v7x, 256 devices: a whole 4x4x8 slice. The times are simulated.
256 devices in a mesh: dp: 32 (over x_hi, z, core), tensor: 8 (over x_lo, y).
Axes of the slice: x: 4 (x_hi: 2, x_lo: 2; x = x_hi * 2 + x_lo), y: 4, z: 8, core: 2. Of those that a mesh axis runs over, the one named last changes fastest.
Arguments:
- hidden: bfloat16 [10240, 18432], P('dp', 'tensor'), may hold values from -6 to 6
- fixed_down_weight: bfloat16 [18432, 4608], P('tensor', 'dp'), may hold values from -4 to 4
- lowrank_factor_b: bfloat16 [18432, 16], P('tensor'), may hold values from -0.046875 to 0.046875
- lowrank_factor_a: bfloat16 [16, 4608], P(None, 'dp'), may hold values from -1.5 to 1.5
- magnitude: float32 [4608], P('tensor'), may hold values from 0.5 to 2
- cotangent: bfloat16 [10240, 4608], P('dp', 'tensor'), may hold values from -0.05908203 to 0.05908203
Outputs:
- mixed: bfloat16 [10240, 4608], P('dp', 'tensor')
- gradient_column_scale: float32 [4608], P(('tensor', 'dp'))
- gradient_factor_a: float32 [16, 4608], P(None, ('tensor', 'dp'))
- gradient_factor_b: float32 [18432, 16], P(('tensor', 'dp'))
All inputs are finite; a program needn't handle non-finite values.
Results may differ from a plain program's by a relative error of at most 0.0054.
Values may be sent and summed in bfloat16 or wider, within the bound.
A program may use at most 128 MiB of HBM per device.

v0:
```python
import jax
import jax.numpy as jnp
from jax import lax
from jax.sharding import PartitionSpec as P


def copy_for_each(array, axis):
    copies = jnp.broadcast_to(array, (lax.axis_size(axis), *array.shape))
    return lax.all_to_all(copies, axis, split_axis=0, concat_axis=0, tiled=True)


def taken_together(array, axis):
    return copy_for_each(array, axis).sum(axis=0)


def packed_total(arrays, axis):
    ends = [0]
    for a in arrays:
        ends.append(ends[-1] + a.size)
    so_far = taken_together(jnp.concatenate([a.ravel() for a in arrays]), axis)
    return tuple((so_far[b:e].reshape(a.shape) for a, b, e in zip(arrays, ends, ends[1:])))


def joined_along(pieces, dim):
    lengths = list(pieces.shape[1:])
    lengths[dim] *= pieces.shape[0]
    return jnp.moveaxis(pieces, 0, dim).reshape(lengths)


def collect(array, axis, dim):
    return joined_along(copy_for_each(array, axis), dim)


def rows_first(arrays, axis, dims):
    turned = [jnp.moveaxis(a, dim, 0) for a, dim in zip(arrays, dims)]
    both = jnp.concatenate([t.reshape(len(t), -1) for t in turned], axis=1)
    result, at, done = (lax.all_gather(both, axis, axis=0, tiled=True), 0, [])
    for t, dim in zip(turned, dims):
        piece = result[:, at : at + t[0].size].reshape(-1, *t.shape[1:])
        done.append(jnp.moveaxis(piece, 0, dim))
        at += t[0].size
    return tuple(done)


def in_blocks(array, dim, length):
    lengths = array.shape
    pieces = array.reshape(*lengths[:dim], length, lengths[dim] // length, *lengths[dim + 1 :])
    return jnp.moveaxis(pieces, dim, 0)


def sum_at_owner(array, axis, dim):
    length = lax.axis_size(axis)
    pieces = lax.all_to_all(in_blocks(array, dim, length), axis, 0, 0, tiled=True)
    return jnp.sum(pieces.astype(jnp.float32), axis=0)


def summed_on_arrival(array, axis, dim):
    pieces = in_blocks(array, dim, lax.axis_size(axis))
    arrived = lax.all_to_all(pieces, axis, split_axis=0, concat_axis=0, tiled=True)
    return arrived.sum(axis=0)


def body(hidden, fixed_down_weight, lowrank_factor_b, lowrank_factor_a, magnitude, cotangent):
    rank = lowrank_factor_b.shape[1]
    dp_count = lax.axis_size("dp")
    out_cols = magnitude.shape[0]
    own = lax.axis_index("tensor")
    lowrank_portion = jnp.dot(hidden, lowrank_factor_b, preferred_element_type=jnp.float32)
    combined_weight = fixed_down_weight.astype(jnp.float32) + jnp.dot(
        lowrank_factor_b, lowrank_factor_a, preferred_element_type=jnp.float32
    )
    local_sq = jnp.sum(combined_weight * combined_weight, axis=0)
    low_full, block_sq = packed_total((lowrank_portion, local_sq), "tensor")
    col_sq = collect(block_sq, "dp", 0)
    sq_len = 1
    prod_shape = (1, 1)
    products = jnp.zeros(prod_shape, jnp.float32)
    squares = jnp.zeros((sq_len,), jnp.float32)
    w_piece, factor_a_slice = rows_first((fixed_down_weight, lowrank_factor_a), "dp", (1, 1))
    full_a = factor_a_slice
    products, squares, full_a, full_w = (products, squares, full_a, w_piece)
    column_norm_values = jnp.sqrt(col_sq + 1e-06)
    own_norms = lax.dynamic_slice_in_dim(column_norm_values, own * out_cols, out_cols, 0)
    scale = magnitude / own_norms
    lowrank_block_update = low_full.astype(jnp.bfloat16)
    summed = sum_at_owner(
        lax.dot_general(
            full_w, hidden, (((0,), (1,)), ((), ())), preferred_element_type=jnp.float32
        ).astype(jnp.bfloat16),
        "tensor",
        0,
    ).T
    own_a = lax.dynamic_slice_in_dim(full_a, own * out_cols, out_cols, 1)
    prenorm_output = summed + jnp.dot(
        lowrank_block_update, own_a, preferred_element_type=jnp.float32
    )
    mixed = (prenorm_output * scale).astype(jnp.bfloat16)
    cot = cotangent.astype(jnp.float32)
    mag_part = jnp.sum(cot * prenorm_output, axis=0) / own_norms
    prenorm_gradient_b = (cot * scale).astype(jnp.bfloat16)
    factor_a_portion = jnp.dot(
        lowrank_block_update.T, prenorm_gradient_b, preferred_element_type=jnp.float32
    )
    back_part = jnp.dot(prenorm_gradient_b, own_a.T, preferred_element_type=jnp.float32)
    backward_factor_b = taken_together(back_part, "tensor").astype(jnp.bfloat16)
    b_part = jnp.dot(hidden.T, backward_factor_b, preferred_element_type=jnp.float32)
    piece_cols = out_cols // dp_count
    piece_rows = b_part.shape[0] // dp_count
    stacked = jnp.concatenate(
        [
            mag_part.reshape(dp_count, piece_cols),
            factor_a_portion.reshape(rank, dp_count, piece_cols)
            .transpose(1, 0, 2)
            .reshape(dp_count, rank * piece_cols),
            b_part.reshape(dp_count, piece_rows * rank),
        ],
        axis=1,
    )
    reduced = summed_on_arrival(stacked, "dp", 0)
    gradient_column_scale = reduced[0, :piece_cols]
    gradient_factor_a = reduced[0, piece_cols : piece_cols + rank * piece_cols].reshape(
        rank, piece_cols
    )
    gradient_factor_b = reduced[0, piece_cols + rank * piece_cols :].reshape(piece_rows, rank)
    return (mixed, gradient_column_scale, gradient_factor_a, gradient_factor_b)


def solution(mesh):
    return jax.shard_map(
        body,
        mesh=mesh,
        in_specs=(
            P("dp", "tensor"),
            P("tensor", "dp"),
            P("tensor", None),
            P(None, "dp"),
            P("tensor"),
            P("dp", "tensor"),
        ),
        out_specs=(
            P("dp", "tensor"),
            P(("tensor", "dp")),
            P(None, ("tensor", "dp")),
            P(("tensor", "dp"), None),
        ),
        check_vma=False,
    )
```

profile of v0, /device:TPU:1, one launch (start us, length us, event | category | flops | bytes accessed | tf_op | source)
XLA Modules:
  0.0 289.1 jit_solution(13136544855917260526)
XLA Ops:
  7.2 0.9 copy.50
  8.2 2.0 pad_maximum_fusion
  10.2 0.5 fusion.21
  10.7 0.1 reshape.60
  10.8 0.4 copy-done.3
  11.2 0.5 fusion.6
  11.7 0.1 broadcast_in_dim.11
  11.8 11.4 %all_to_all.27 = f32[8,1,5264]{2,1,0:T(1,128)S(1)} all-to-all(f32[8,1,5264]{2,1,0:T(1,128)S(1)} %broadcast_in_dim.11), channel_id=1, replica_groups=mesh['dp'=32,'tensor'=8] {'tensor'}, dimensions={0} | all-to-all | bytes 336896 | tf_op jit(solution)/shard_map/all_to_all | solution.py:9
  23.3 0.1 reduce_sum.58
  23.4 0.6 broadcast_in_dim.12
  24.0 12.9 %all-to-all-start.2 = ((f32[32,1,144]{2,1,0:T(1,128)}), f32[32,1,144]{2,1,0:T(1,128)S(1)}, u32[]{:S(2)}, u32[]{:S(2)}) async-start(f32[32,1,144]{2,1,0:T(1,128)} %broadcast_in_dim.12), calls=%async_computation.2 | async-start | bytes 65536 | tf_op jit(solution)/shard_map/all_to_all | solution.py:9
  36.9 9.4 %all-to-all-done.2 = f32[32,1,144]{2,1,0:T(1,128)S(1)} async-done(((f32[32,1,144]{2,1,0:T(1,128)}), f32[32,1,144]{2,1,0:T(1,128)S(1)}, u32[]{:S(2)}, u32[]{:S(2)}) %all-to-all-start.2) | async-done | bytes 18464 | tf_op jit(solution)/shard_map/all_to_all | solution.py:9
  46.3 0.2 sqrt_reduce_fusion
  46.5 0.1 sqrt.7
  46.6 0.1 dynamic-slice_divide_fusion.1
  46.7 134.5 %all-gather.2.cloned.1.call-done = bf16[4608,2320]{1,0:T(8,128)(2,1)} async-done(((bf16[144,2320]{1,0:T(8,128)(2,1)}), bf16[4608,2320]{1,0:T(8,128)(2,1)}) %all-gather.2.cloned.1.call-update) | async-done | bytes 21381136 | tf_op jit(solution)/shard_map/all_gather | solution.py:37
  181.1 1.3 slice.43
  182.5 1.1 copy-done.1
  183.6 0.2 fusion.10
  183.8 0.7 broadcast_in_dim.13
  184.5 4.0 %all-to-all-start.3 = ((f32[8,320,16]{1,2,0:T(8,128)}), f32[8,320,16]{1,2,0:T(8,128)S(1)}, u32[]{:S(2)}, u32[]{:S(2)}) async-start(f32[8,320,16]{1,2,0:T(8,128)} %broadcast_in_dim.13), calls=%async_computation.3 | async-start | bytes 393216 | tf_op jit(solution)/shard_map/all_to_all | solution.py:9
  188.6 12.5 %fusion.2 = bf16[4608,320]{0,1:T(8,128)(2,1)} fusion(bf16[320,2304]{1,0:T(8,128)(2,1)S(1)} %copy-done, bf16[4608,2320]{1,0:T(8,128)(2,1)} %all-gather.2.cloned.1.call-done), kind=kOutput, calls=%fused_computation.2 | convolution fusion | flops 6796247040 | bytes 25657344 | tf_op jit(solution)/shard_map/dot_general | solution.py:87
  201.0 6.3 %reshape.59 = bf16[8,576,320]{1,0,2:T(8,128)(2,1)} reshape(bf16[4608,320]{0,1:T(8,128)(2,1)} %fusion.2) | data formatting | bytes 5898240 | tf_op jit(solution)/shard_map/reshape | solution.py:47
  207.3 4.1 %copy.51 = bf16[8,576,320]{1,2,0:T(8,128)(2,1)} copy(bf16[8,576,320]{1,0,2:T(8,128)(2,1)} %reshape.59) | data formatting | bytes 5898240 | tf_op jit(solution)/shard_map/reshape | solution.py:47
  211.3 5.1 %all-to-all-start = ((bf16[8,576,320]{1,2,0:T(8,128)(2,1)}), bf16[8,576,320]{1,2,0:T(8,128)(2,1)}, u32[]{:S(2)}, u32[]{:S(2)}) async-start(bf16[8,576,320]{1,2,0:T(8,128)(2,1)} %copy.51), calls=%async_computation | async-start | bytes 6553600 | tf_op jit(solution)/shard_map/all_to_all | solution.py:53
  216.5 0.1 convert_element_type.32
  216.6 0.3 convolution_bitcast_fusion
  216.9 0.4 copy.58
  217.3 0.4 reshape.63
  217.7 37.8 %all-to-all-done = bf16[8,576,320]{1,2,0:T(8,128)(2,1)} async-done(((bf16[8,576,320]{1,2,0:T(8,128)(2,1)}), bf16[8,576,320]{1,2,0:T(8,128)(2,1)}, u32[]{:S(2)}, u32[]{:S(2)}) %all-to-all-start) | async-done | bytes 2949152 | tf_op jit(solution)/shard_map/all_to_all | solution.py:53
  255.4 2.5 convert_reduce_fusion
  258.0 2.0 fusion.7
  260.0 0.1 dynamic-slice_divide_fusion
  260.1 0.1 reshape.61
  260.2 0.2 copy.54
  260.4 0.2 dot_general.32
  260.6 0.5 convolution_bitcast_fusion.1
  261.1 0.2 copy.57
  261.3 0.2 reshape.62
  261.5 0.1 concatenate.11
  261.6 0.2 copy.59
  261.8 18.1 %all_to_all.28 = f32[32,1,1458]{2,1,0:T(1,128)S(1)} all-to-all(f32[32,1,1458]{2,1,0:T(1,128)S(1)} %copy.59), channel_id=1, replica_groups=mesh['dp'=32,'tensor'=8] {'dp'}, dimensions={0} | all-to-all | bytes 373248 | tf_op jit(solution)/shard_map/all_to_all | solution.py:59
  280.0 0.1 reduce_sum.61
  280.1 0.5 slice_bitcast_fusion
  280.6 0.1 slice_reduce_fusion.1
  280.7 0.1 slice_reduce_fusion
  280.8 0.7 reshape_squeeze.6
  281.6 0.7 copy.60
  (21 shorter events, 0.2 us)
Async XLA Ops:
  7.2 3.0 %copy-start = (bf16[320,2304]{1,0:T(8,128)(2,1)S(1)}, bf16[320,2304]{1,0:T(8,128)(2,1)}, u32[]{:S(2)}) copy-start(bf16[320,2304]{1,0:T(8,128)(2,1)} %param.6) | copy-start | bytes 4423684
  7.2 3.0 %copy-start.6 = (bf16[2304,16]{0,1:T(8,128)(2,1)S(1)}, bf16[2304,16]{0,1:T(8,128)(2,1)}, u32[]{:S(2)}) copy-start(bf16[2304,16]{0,1:T(8,128)(2,1)} %param.8) | copy-start | bytes 221188
  7.2 174.0 %all-gather.2.cloned.1.call-start = ((), (), s32[]{:S(2)}) async-start(), calls=%async_computation.5 | async-start | bytes 23113728 | tf_op jit(solution)/shard_map/all_gather | solution.py:37
  10.2 1.1 copy-start.3
  10.2 1.1 copy-start.4
  10.7 35.8 %copy-start.5 = (f32[576]{0:T(1024)S(1)}, f32[576]{0:T(1024)}, u32[]{:S(2)}) copy-start(f32[576]{0:T(1024)} %param.10) | copy-start | bytes 6916
  23.3 160.3 %copy-start.2 = (bf16[320,576]{1,0:T(8,128)(2,1)S(1)}, bf16[320,576]{1,0:T(8,128)(2,1)}, u32[]{:S(2)}) copy-start(bf16[320,576]{1,0:T(8,128)(2,1)} %param.11) | copy-start | bytes 1105924
  24.0 22.3 %all-to-all-start.2 = ((f32[32,1,144]{2,1,0:T(1,128)}), f32[32,1,144]{2,1,0:T(1,128)S(1)}, u32[]{:S(2)}, u32[]{:S(2)}) async-start(f32[32,1,144]{2,1,0:T(1,128)} %broadcast_in_dim.12), calls=%async_computation.2 | async-start | bytes 65536 | tf_op jit(solution)/shard_map/all_to_all | solution.py:9
  182.5 1.1 copy-start.1
  184.5 26.8 %all-to-all-start.3 = ((f32[8,320,16]{1,2,0:T(8,128)}), f32[8,320,16]{1,2,0:T(8,128)S(1)}, u32[]{:S(2)}, u32[]{:S(2)}) async-start(f32[8,320,16]{1,2,0:T(8,128)} %broadcast_in_dim.13), calls=%async_computation.3 | async-start | bytes 393216 | tf_op jit(solution)/shard_map/all_to_all | solution.py:9
  211.3 44.1 %all-to-all-start = ((bf16[8,576,320]{1,2,0:T(8,128)(2,1)}), bf16[8,576,320]{1,2,0:T(8,128)(2,1)}, u32[]{:S(2)}, u32[]{:S(2)}) async-start(bf16[8,576,320]{1,2,0:T(8,128)(2,1)} %copy.51), calls=%async_computation | async-start | bytes 6553600 | tf_op jit(solution)/shard_map/all_to_all | solution.py:53
Sparse Core Ops, SparseCore 0:
  10.7 170.4 all-gather.1
where the time goes:
time: 290 us; the launch traced here: 289 us
  waiting for transfers between devices  182 us (63%)
  blocking collectives  29.5 us (10%)
  starting transfers between devices  22.1 us (8%)
  local copies, waits for them, and re-layouts  19.9 us (7%)
  matrix products  16.5 us (6%)
  between operations  14.3 us (5%)
  other arithmetic  5.14 us (2%)
    all_gather x1, waiting for transfers between devices, rows_first(): result, at, done = (lax.all_gather(both, axis, axis=0, tiled=True), 0, [])  134 us
    all_to_all x1, waiting for transfers between devices, sum_at_owner(): lax.all_to_all(in_blocks(array, dim, length), axis, 0, 0, tiled=True)  37.8 us
    all_to_all x1, blocking collectives, summed_on_arrival(): lax.all_to_all(pieces, axis, split_axis=0, concat_axis=0, tiled=True)  18.1 us
    all_to_all x2, starting transfers between devices, copy_for_each(): return lax.all_to_all(copies, axis, split_axis=0, concat_axis=0, tiled=True)  16.9 us
    dot_general x1, matrix products, body(): lax.dot_general(full_w, hidden, (((0,), (1,)), ((), ())), preferred_eleme...  12.5 us
    all_to_all x1, blocking collectives, copy_for_each(): return lax.all_to_all(copies, axis, split_axis=0, concat_axis=0, tiled=True)  11.4 us
    reshape x3, local copies, waits for them, and re-layouts, in_blocks(): array.reshape(*lengths[:dim], length, lengths[dim] // length, *lengths[di...  10.5 us
    all_to_all x2, waiting for transfers between devices, copy_for_each(): return lax.all_to_all(copies, axis, split_axis=0, concat_axis=0, tiled=True)  9.39 us
  transfers between devices with their start and end apart: 4, of which 3 were waited for; matrix products, arithmetic and copies ran while one was open for 9% of the time, Pallas kernels for 0%

commit v1 on v0

--- a/solution.py
+++ b/solution.py
@@ -1,7 +1,224 @@
+import functools
+
 import jax
 import jax.numpy as jnp
 from jax import lax
+from jax.experimental import pallas as pl
+from jax.experimental.pallas import tpu as pltpu
 from jax.sharding import PartitionSpec as P
+
+TOK, HID, COLS, OUT = 320, 2304, 144, 576
+MESH = pl.DeviceIdType.MESH
+F32, BF = jnp.float32, jnp.bfloat16
+CHUNKS = ((0, 80), (80, 64))
+
+
+def remote(src, dst, send, recv, dp, tensor):
+    return pltpu.make_async_remote_copy(
+        src_ref=src, dst_ref=dst, send_sem=send, recv_sem=recv,
+        device_id=(dp, tensor), device_id_type=MESH,
+    )
+
+
+def kernel(h_ref, w_ref, out_ref, toks, wts, outgoing, arrived, turned, halves,
+           loc_sem, w_send, w_recv, t_send, t_recv, y_send, y_recv, x_send, x_recv):
+    dp, tensor = lax.axis_index("dp"), lax.axis_index("tensor")
+    x_hi, z, core = dp // 16, (dp // 2) % 8, dp % 2
+    x_lo, y = tensor // 4, tensor % 4
+    other = 1 - core
+
+    def dp_of(a, b, c):
+        return a * 16 + b * 2 + c
+
+    load_h = pltpu.make_async_copy(h_ref, toks.at[0, pl.ds(core * TOK, TOK)], loc_sem.at[0])
+    load_w = pltpu.make_async_copy(w_ref, wts.at[0], loc_sem.at[1])
+    load_h.start()
+    load_w.start()
+
+    barrier = pltpu.get_barrier_semaphore()
+    peers = [(dp_of(x_hi, (z + 1) % 8, core), tensor), (dp_of(x_hi, (z + 7) % 8, core), tensor),
+             (dp_of(x_hi, z, other), tensor)]
+    for k in range(1, 4):
+        for c in range(2):
+            peers.append((dp_of(x_hi, z, c), x_lo * 4 + (y + k) % 4))
+    for k in range(1, 4):
+        xx = (2 * x_hi + x_lo + k) % 4
+        for c in range(2):
+            peers.append((dp_of(xx // 2, z, c), (xx % 2) * 4 + y))
+    for p in peers:
+        pl.semaphore_signal(barrier, inc=1, device_id=p, device_id_type=MESH)
+    pl.semaphore_wait(barrier, len(peers))
+
+    def w_copy(side, k, ch):
+        at, n = CHUNKS[ch]
+        src = 0 if k == 1 else 2 * (k - 1) - 1 + side
+        dst = 7 if k == 4 else 2 * k - 1 + side
+        to = (z + 1) % 8 if side == 0 else (z + 7) % 8
+        return remote(wts.at[src, pl.ds(at, n)], wts.at[dst, pl.ds(at, n)],
+                      w_send.at[side, k - 1, ch], w_recv.at[dst, ch], dp_of(x_hi, to, core), tensor)
+
+    load_w.wait()
+    w_copy(0, 1, 0).start()
+    w_copy(1, 1, 1).start()
+    w_copy(0, 1, 1).start()
+    w_copy(1, 1, 0).start()
+    load_h.wait()
+    mine = pl.ds(core * TOK, TOK)
+    own_tok = toks.at[0, mine]
+    to_other = remote(own_tok, toks.at[0, mine], t_send.at[0], t_recv.at[0], dp_of(x_hi, z, other), tensor)
+    to_far = remote(own_tok, toks.at[1, mine], t_send.at[1], t_recv.at[1], dp_of(1 - x_hi, z, core), tensor)
+    relay = remote(toks.at[1, mine], toks.at[1, mine], t_send.at[2], t_recv.at[2], dp_of(x_hi, z, other), tensor)
+    to_other.start()
+    to_far.start()
+
+    def zsrc_of(j):
+        k = (j + 1) // 2
+        return (z + 8 + k - 2 * k * (j % 2)) % 8
+
+    def y_copy(j, g):
+        zs = zsrc_of(j)
+        return remote(outgoing.at[j, g], arrived.at[y, zs % 2, core], y_send.at[j, g],
+                      y_recv.at[y, zs % 2, core], dp_of(x_hi, z, g), x_lo * 4 + zs // 2)
+
+    def local(j, g):
+        return jnp.logical_and(zsrc_of(j) // 2 == y, core == g)
+
+    def item(j, g):
+        p = lax.dot_general(toks[g], wts[j], (((1,), (1,)), ((), ())), preferred_element_type=F32)
+        p = p.T.astype(BF)
+        here = local(j, g)
+
+        @pl.when(here)
+        def _():
+            arrived[y, zsrc_of(j) % 2, core] = p
+
+        @pl.when(jnp.logical_not(here))
+        def _():
+            outgoing[j, g] = p
+            y_copy(j, g).start()
+
+    def items(lo, hi, g):
+        def body(j, carry):
+            item(j, g)
+            return carry
+        lax.fori_loop(lo, hi, body, 0)
+
+    to_other.wait_recv()
+    items(0, 1, 0)
+    for k in (1, 2, 3):
+        for first in (0, 1):
+            for side in (0, 1):
+                ch = first if side == 0 else 1 - first
+                w_copy(side, k, ch).wait_recv()
+                if k < 3 or first == 0:
+                    w_copy(side, k + 1, ch).start()
+        items(2 * k - 1, 2 * k + 1, 0)
+        if k == 2:
+            to_far.wait_recv()
+            relay.start()
+            relay.wait_recv()
+            items(0, 5, 1)
+    items(5, 7, 1)
+    w_copy(0, 4, 0).wait_recv()
+    w_copy(1, 4, 1).wait_recv()
+    items(7, 8, 0)
+    items(7, 8, 1)
+
+    tok_hi = jnp.where(core == 0, x_hi, 1 - x_hi)
+
+    def x_copy(zp, ct):
+        return remote(turned.at[zp, pl.ds(ct * TOK, TOK)], halves.at[x_lo, zp], x_send.at[zp, ct],
+                      x_recv.at[x_lo, zp], dp_of(tok_hi, z, ct), x_hi * 4 + y)
+
+    def to_self(ct):
+        return jnp.logical_and(jnp.logical_and(tok_hi == x_hi, x_lo == x_hi), core == ct)
+
+    for zp in range(2):
+        parts = []
+        for cs in range(2):
+            for k in range(4):
+                ys = (y + k) % 4
+                away = jnp.logical_or(k > 0, core != cs)
+
+                def arrive(ys=ys, cs=cs):
+                    remote(outgoing.at[0, 0], arrived.at[ys, zp, cs], y_send.at[0, 0], y_recv.at[ys, zp, cs],
+                           dp, tensor).wait_recv()
+                if k == 0:
+                    pl.when(core != cs)(arrive)
+                else:
+                    arrive()
+            total = arrived[0, zp, cs].astype(F32)
+            for ys in range(1, 4):
+                total = total + arrived[ys, zp, cs].astype(F32)
+            parts.append(total)
+        both = jnp.concatenate(parts, axis=0).T.astype(BF)
+        turned[zp] = both
+        for ct in range(2):
+            @pl.when(to_self(ct))
+            def _():
+                halves[x_lo, zp] = both[ct * TOK:(ct + 1) * TOK]
+
+            @pl.when(jnp.logical_not(to_self(ct)))
+            def _():
+                x_copy(zp, ct).start()
+
+    for zp in range(2):
+        for xl in range(2):
+            sx_hi = x_lo
+            score = jnp.where(sx_hi == x_hi, 0, 1)
+            own = jnp.logical_and(jnp.logical_and(sx_hi == x_hi, xl == x_lo), score == core)
+
+            @pl.when(jnp.logical_not(own))
+            def _():
+                remote(turned.at[0, pl.ds(0, TOK)], halves.at[xl, zp], x_send.at[0, 0], x_recv.at[xl, zp],
+                       dp, tensor).wait_recv()
+        out_ref[:, zp * 288:(zp + 1) * 288] = halves[0, zp].astype(F32) + halves[1, zp].astype(F32)
+
+    for k in (1, 2, 3, 4):
+        for side in (0, 1):
+            for ch in (0, 1):
+                if k < 4 or ch == side:
+                    w_copy(side, k, ch).wait_send()
+    to_other.wait_send()
+    to_far.wait_send()
+    relay.wait_send()
+    def drain(j, carry):
+        for g in range(2):
+            @pl.when(jnp.logical_not(local(j, g)))
+            def _():
+                y_copy(j, g).wait_send()
+        return carry
+    lax.fori_loop(0, 8, drain, 0)
+    for zp in range(2):
+        for ct in range(2):
+            @pl.when(jnp.logical_not(to_self(ct)))
+            def _():
+                x_copy(zp, ct).wait_send()
+
+
+def products(hidden, w_turned):
+    any_spec = pl.BlockSpec(memory_space=pl.ANY)
+    dma = pltpu.SemaphoreType.DMA
+    return pl.pallas_call(
+        kernel,
+        name="products",
+        out_shape=jax.ShapeDtypeStruct((TOK, OUT), F32),
+        in_specs=[any_spec, any_spec],
+        out_specs=pl.BlockSpec(memory_space=pltpu.VMEM),
+        scratch_shapes=[
+            pltpu.VMEM((2, 2 * TOK, HID), BF),
+            pltpu.VMEM((8, COLS, HID), BF),
+            pltpu.VMEM((8, 2, COLS, 2 * TOK), BF),
+            pltpu.VMEM((4, 2, 2, COLS, 2 * TOK), BF),
+            pltpu.VMEM((2, 2 * TOK, 288), BF),
+            pltpu.VMEM((2, 2, TOK, 288), BF),
+            dma((2,)), dma((2, 4, 2)), dma((8, 2)), dma((3,)), dma((3,)),
+            dma((8, 2)), dma((4, 2, 2)), dma((2, 2)), dma((2, 2)),
+        ],
+        compiler_params=pltpu.CompilerParams(
+            collective_id=0, has_side_effects=True, vmem_limit_bytes=48 * 1024 * 1024
+        ),
+    )(hidden, w_turned)
 
 
 def copy_for_each(array, axis):
@@ -72,24 +289,12 @@
     local_sq = jnp.sum(combined_weight * combined_weight, axis=0)
     low_full, block_sq = packed_total((lowrank_portion, local_sq), "tensor")
     col_sq = collect(block_sq, "dp", 0)
-    sq_len = 1
-    prod_shape = (1, 1)
-    products = jnp.zeros(prod_shape, jnp.float32)
-    squares = jnp.zeros((sq_len,), jnp.float32)
-    w_piece, factor_a_slice = rows_first((fixed_down_weight, lowrank_factor_a), "dp", (1, 1))
-    full_a = factor_a_slice
-    products, squares, full_a, full_w = (products, squares, full_a, w_piece)
+    full_a = lax.all_gather(lowrank_factor_a, "dp", axis=1, tiled=True)
     column_norm_values = jnp.sqrt(col_sq + 1e-06)
     own_norms = lax.dynamic_slice_in_dim(column_norm_values, own * out_cols, out_cols, 0)
     scale = magnitude / own_norms
     lowrank_block_update = low_full.astype(jnp.bfloat16)
-    summed = sum_at_owner(
-        lax.dot_general(
-            full_w, hidden, (((0,), (1,)), ((), ())), preferred_element_type=jnp.float32
-        ).astype(jnp.bfloat16),
-        "tensor",
-        0,
-    ).T
+    summed = products(hidden, fixed_down_weight.T)
     own_a = lax.dynamic_slice_in_dim(full_a, own * out_cols, out_cols, 1)
     prenorm_output = summed + jnp.dot(
         lowrank_block_update, own_a, preferred_element_type=jnp.float32

time: 290 us -> 210 us (0.72)
  waiting for transfers between devices: 182 us -> 4.9 us
  Pallas kernels: 0 us -> 72.6 us
  blocking collectives: 29.5 us -> 69.7 us
  starting transfers between devices: 22.1 us -> 46.7 us
  between operations: 14.3 us -> 0.87 us
  local copies, waits for them, and re-layouts: 19.9 us -> 7.74 us
  matrix products: 16.5 us -> 6.01 us
  other arithmetic: 5.14 us -> 0.62 us
    all_gather x1 -> x0, waiting for transfers between devices: 134 us -> none  [rows_first(): result, at, done = (lax.all_gather(both, axis, axis=0, tiled=True), 0, [])]
    pallas_call x0 -> x1, Pallas kernels: none -> 72.6 us  [products(): pl.pallas_call(kernel, name='products', out_shape=jax.ShapeDtypeStruct((T...]
    all_gather x0 -> x1, blocking collectives: none -> 42.6 us  [body(): full_a = lax.all_gather(lowrank_factor_a, 'dp', axis=1, tiled=True)]
    all_to_all x1 -> x0, waiting for transfers between devices: 37.8 us -> none  [sum_at_owner(): lax.all_to_all(in_blocks(array, dim, length), axis, 0, 0, tiled=True)]
    all_to_all x2, starting transfers between devices: 16.9 us -> 46.7 us  [copy_for_each(): return lax.all_to_all(copies, axis, split_axis=0, concat_axis=0, tiled=True)]
    dot_general x1 -> x0, matrix products: 12.5 us -> none  [body(): lax.dot_general(full_w, hidden, (((0,), (1,)), ((), ())), preferred_eleme...]
    reshape x3 -> x1, local copies, waits for them, and re-layouts: 10.5 us -> 0.2 us  [in_blocks(): array.reshape(*lengths[:dim], length, lengths[dim] // length, *lengths[di...]
    all_to_all x1 -> x0, starting transfers between devices: 5.14 us -> none  [sum_at_owner(): lax.all_to_all(in_blocks(array, dim, length), axis, 0, 0, tiled=True)]
  transfers between devices with their start and end apart: 4 -> 2, of which waited for: 3 -> 1; matrix products, arithmetic and copies ran while one was open for 9% -> 1% of each run, Pallas kernels for 0% -> 35%
where the time goes in v1:
time: 210 us; the launch traced here: 209 us
  Pallas kernels  72.6 us (35%)
  blocking collectives  69.7 us (33%)
  starting transfers between devices  46.7 us (22%)
  local copies, waits for them, and re-layouts  7.74 us (4%)
  matrix products  6.01 us (3%)
  waiting for transfers between devices  4.9 us (2%)
    pallas_call x1, Pallas kernels, products(): pl.pallas_call(kernel, name='products', out_shape=jax.ShapeDtypeStruct((T...  72.6 us
    all_to_all x2, starting transfers between devices, copy_for_each(): return lax.all_to_all(copies, axis, split_axis=0, concat_axis=0, tiled=True)  46.7 us
    all_gather x1, blocking collectives, body(): full_a = lax.all_gather(lowrank_factor_a, 'dp', axis=1, tiled=True)  42.6 us
    all_to_all x1, blocking collectives, summed_on_arrival(): lax.all_to_all(pieces, axis, split_axis=0, concat_axis=0, tiled=True)  15.6 us
    all_to_all x1, blocking collectives, copy_for_each(): return lax.all_to_all(copies, axis, split_axis=0, concat_axis=0, tiled=True)  11.4 us
    all_to_all x2, waiting for transfers between devices, copy_for_each(): return lax.all_to_all(copies, axis, split_axis=0, concat_axis=0, tiled=True)  4.9 us
  transfers between devices with their start and end apart: 2, of which 1 were waited for; matrix products, arithmetic and copies ran while one was open for 1% of the time, Pallas kernels for 35%

profile of v1, /device:TPU:1, one launch (start us, length us, event | category | flops | bytes accessed | tf_op | source)
XLA Modules:
  0.0 209.1 jit_solution(5011806809720857325)
XLA Ops:
  0.6 0.0 copy-start
  0.6 0.0 copy-start.2
  0.7 0.9 copy-done
  1.5 1.9 fusion.16
  3.4 0.1 reshape.56
  3.5 0.0 copy-done.2
  3.5 0.0 copy-done.4
  3.5 0.0 copy-start.1
  3.5 0.5 fusion.1
  4.0 0.1 broadcast_in_dim.11
  4.1 11.4 %all_to_all.22 = f32[8,1,5264]{2,1,0:T(1,128)S(1)} all-to-all(f32[8,1,5264]{2,1,0:T(1,128)S(1)} %broadcast_in_dim.11), channel_id=1, replica_groups=mesh['dp'=32,'tensor'=8] {'tensor'}, dimensions={0} | all-to-all | bytes 336896 | tf_op jit(solution)/shard_map/all_to_all | solution.py:226
  15.6 0.1 reduce_sum.48
  15.7 0.6 broadcast_in_dim.12
  16.3 12.9 %all-to-all-start.1 = ((f32[32,1,144]{2,1,0:T(1,128)}), f32[32,1,144]{2,1,0:T(1,128)S(1)}, u32[]{:S(2)}, u32[]{:S(2)}) async-start(f32[32,1,144]{2,1,0:T(1,128)} %broadcast_in_dim.12), calls=%async_computation.1 | async-start | bytes 65536 | tf_op jit(solution)/shard_map/all_to_all | solution.py:226
  29.2 42.6 %all-gather = bf16[32,144,16]{1,2,0:T(8,128)(2,1)S(1)} all-gather(bf16[1,144,16]{1,2,0:T(8,128)(2,1)S(1)} %bitcast.27), channel_id=1, replica_groups=mesh['dp'=32,'tensor'=8] {'dp'}, dimensions={0}, use_global_device_ids=true | all-gather | bytes 152064 | tf_op jit(solution)/shard_map/all_gather | solution.py:292
  71.8 0.1 copy.48
  71.9 1.0 reshape.62
  72.9 72.6 %products.1 = f32[320,576]{1,0:T(8,128)S(1)} custom-call(bf16[320,2304]{1,0:T(8,128)(2,1)S(1)} %copy-done.1, bf16[144,2304]{1,0:T(8,128)(2,1)S(1)} %bitcast.25), custom_call_target="tpu_custom_call" | custom-call | tf_op jit(solution)/shard_map/products/pallas_call | solution.py:202
  145.5 0.1 convert_element_type.24
  145.6 0.0 all-to-all-done.1
  145.6 0.2 sqrt_reduce_fusion
  145.8 0.1 sqrt.7
  145.9 0.1 dynamic-slice_divide_fusion.1
  146.0 0.9 fusion.5
  146.9 1.9 fusion.2
  148.9 0.1 dynamic-slice_divide_fusion
  148.9 0.1 reshape.57
  149.0 0.2 copy.49
  149.3 0.2 dot_general.28
  149.5 0.7 broadcast_in_dim.13
  150.2 33.8 %all-to-all-start.2 = ((f32[8,320,16]{1,2,0:T(8,128)}), f32[8,320,16]{1,2,0:T(8,128)S(1)}, u32[]{:S(2)}, u32[]{:S(2)}) async-start(f32[8,320,16]{1,2,0:T(8,128)} %broadcast_in_dim.13), calls=%async_computation.2 | async-start | bytes 393216 | tf_op jit(solution)/shard_map/all_to_all | solution.py:226
  184.0 0.5 convolution_bitcast_fusion.1
  184.5 0.2 copy.52
  184.7 0.2 reshape.58
  184.8 4.9 %all-to-all-done.2 = f32[8,320,16]{1,2,0:T(8,128)S(1)} async-done(((f32[8,320,16]{1,2,0:T(8,128)}), f32[8,320,16]{1,2,0:T(8,128)S(1)}, u32[]{:S(2)}, u32[]{:S(2)}) %all-to-all-start.2) | async-done | bytes 163872 | tf_op jit(solution)/shard_map/all_to_all | solution.py:226
  189.8 0.3 convolution_bitcast_fusion
  190.1 0.4 copy.53
  190.5 0.4 reshape.59
  190.8 0.1 concatenate.7
  191.0 0.2 copy.54
  191.2 15.6 %all_to_all.23 = f32[32,1,1458]{2,1,0:T(1,128)S(1)} all-to-all(f32[32,1,1458]{2,1,0:T(1,128)S(1)} %copy.54), channel_id=1, replica_groups=mesh['dp'=32,'tensor'=8] {'dp'}, dimensions={0} | all-to-all | bytes 373248 | tf_op jit(solution)/shard_map/all_to_all | solution.py:276
  206.8 0.1 reduce_sum.51
  206.9 0.1 slice_reduce_fusion
  207.0 0.1 slice_reduce_fusion.1
  207.1 0.5 slice_bitcast_fusion
  207.6 0.1 reshape_squeeze.7
  207.7 0.7 copy.55
  208.4 0.7 reshape_squeeze.6
  (11 shorter events, 0.1 us)
Async XLA Ops:
  0.6 0.9 copy-start
  0.6 2.9 %copy-start.2 = (bf16[2304,144]{0,1:T(8,128)(2,1)S(1)}, bf16[2304,144]{0,1:T(8,128)(2,1)}, u32[]{:S(2)}) copy-start(bf16[2304,144]{0,1:T(8,128)(2,1)} %param.7) | copy-start | bytes 1990660
  0.7 2.9 %copy-start.4 = (bf16[16,144]{1,0:T(8,128)(2,1)S(1)}, bf16[16,144]{1,0:T(8,128)(2,1)}, u32[]{:S(2)}) copy-start(bf16[16,144]{1,0:T(8,128)(2,1)} %param.9) | copy-start | bytes 13828
  3.5 69.4 %copy-start.1 = (bf16[320,2304]{1,0:T(8,128)(2,1)S(1)}, bf16[320,2304]{1,0:T(8,128)(2,1)}, u32[]{:S(2)}) copy-start(bf16[320,2304]{1,0:T(8,128)(2,1)} %h_ref.1) | copy-start | bytes 4423684
  16.3 129.3 %all-to-all-start.1 = ((f32[32,1,144]{2,1,0:T(1,128)}), f32[32,1,144]{2,1,0:T(1,128)S(1)}, u32[]{:S(2)}, u32[]{:S(2)}) async-start(f32[32,1,144]{2,1,0:T(1,128)} %broadcast_in_dim.12), calls=%async_computation.1 | async-start | bytes 65536 | tf_op jit(solution)/shard_map/all_to_all | solution.py:226
  72.9 73.0 %copy-start.5 = (f32[576]{0:T(1024)S(1)}, f32[576]{0:T(1024)}, u32[]{:S(2)}) copy-start(f32[576]{0:T(1024)} %param.10) | copy-start | bytes 6916
  72.9 73.1 %copy-start.3 = (bf16[320,576]{1,0:T(8,128)(2,1)S(1)}, bf16[320,576]{1,0:T(8,128)(2,1)}, u32[]{:S(2)}) copy-start(bf16[320,576]{1,0:T(8,128)(2,1)} %param.11) | copy-start | bytes 1105924
  150.2 39.6 %all-to-all-start.2 = ((f32[8,320,16]{1,2,0:T(8,128)}), f32[8,320,16]{1,2,0:T(8,128)S(1)}, u32[]{:S(2)}, u32[]{:S(2)}) async-start(f32[8,320,16]{1,2,0:T(8,128)} %broadcast_in_dim.13), calls=%async_computation.2 | async-start | bytes 393216 | tf_op jit(solution)/shard_map/all_to_all | solution.py:226

commit v2 on v1

v2 whole, which is shorter than its diff:
```python
import functools

import jax
import jax.numpy as jnp
from jax import lax
from jax.experimental import pallas as pl
from jax.experimental.pallas import tpu as pltpu
from jax.sharding import PartitionSpec as P

TOK, HID, COLS, OUT = 320, 2304, 144, 576
MESH = pl.DeviceIdType.MESH
F32, BF = jnp.float32, jnp.bfloat16
CHUNKS = ((0, 80), (80, 64))


def remote(src, dst, send, recv, dp, tensor):
    return pltpu.make_async_remote_copy(
        src_ref=src, dst_ref=dst, send_sem=send, recv_sem=recv,
        device_id=(dp, tensor), device_id_type=MESH,
    )


def kernel(h_ref, w_ref, b_ref, a_ref, mag_ref, cot_ref, mixed_ref, grads_ref, gmag_ref,
           toks, wts, outgoing, arrived, turned, halves,
           sq_out, sq_in, msg_f, msg, msgs, a_all, sq_all, low_in, back_in, low_out, back_out, dpre, extra,
           spread, spread_in, plane, plane_in, mag_out, mag_in,
           loc_sem, w_send, w_recv, t_send, t_recv, y_send, y_recv, x_send, x_recv,
           s_send, s_recv, m_send, m_recv, l_send, l_recv, b_send, b_recv, d_send, d_recv, p_send, p_recv,
           g_send, g_recv):
    dp, tensor = lax.axis_index("dp"), lax.axis_index("tensor")
    x_hi, z, core = dp // 16, (dp // 2) % 8, dp % 2
    x_lo, y = tensor // 4, tensor % 4
    other = 1 - core

    def dp_of(a, b, c):
        return a * 16 + b * 2 + c

    load_h = pltpu.make_async_copy(h_ref, toks.at[0, pl.ds(core * TOK, TOK)], loc_sem.at[0])
    load_w = pltpu.make_async_copy(w_ref, wts.at[0], loc_sem.at[1])
    load_h.start()
    load_w.start()

    barrier = pltpu.get_barrier_semaphore()

    def greet(p):
        pl.semaphore_signal(barrier, inc=1, device_id=p, device_id_type=MESH)

    near = []
    for k in range(1, 4):
        near.append((dp_of(x_hi, z, core), x_lo * 4 + (y + k) % 4))
        near.append((dp_of(x_hi, z, other), x_lo * 4 + (y + k) % 4))
    for k in range(4):
        near.append((dp, (1 - x_lo) * 4 + (y + k) % 4))
    near.append((dp_of(x_hi, z, other), (1 - x_lo) * 4 + y))
    for c in range(2):
        near.append((dp_of(1 - x_hi, z, c), (1 - x_lo) * 4 + y))
    for p in near:
        greet(p)

    def greet_dp(i, carry):
        greet(((dp + i) % 32, tensor))
        return carry
    lax.fori_loop(1, 32, greet_dp, 0)

    mine = pl.ds(pl.multiple_of(core * TOK, TOK), TOK)
    owner = dp // 4
    load_w.wait()
    merged = wts[0].astype(F32) + lax.dot_general(
        a_ref[...], b_ref[...], (((0,), (0,)), ((), ())), preferred_element_type=F32)
    squares = merged * merged
    lanes = squares[:, 0:128]
    for i in range(1, 18):
        lanes = lanes + squares[:, 128 * i:128 * (i + 1)]
    own_sq = jnp.sum(lanes.T, axis=0, keepdims=True)
    sq_row = jnp.broadcast_to(own_sq, (8, COLS))

    @pl.when(owner == tensor)
    def _():
        sq_in[tensor] = sq_row

    @pl.when(owner != tensor)
    def _():
        sq_out[...] = sq_row

    load_h.wait()
    low_part = lax.dot_general(b_ref[...], toks[0, mine], (((1,), (1,)), ((), ())), preferred_element_type=F32)
    low_out[...] = low_part
    low_in[tensor] = low_part
    spread[...] = jnp.zeros_like(spread)
    msg_f[...] = jnp.zeros_like(msg_f)

    pl.semaphore_wait(barrier, len(near) + 31)

    def w_copy(side, k, ch):
        at, n = CHUNKS[ch]
        src = 0 if k == 1 else 2 * (k - 1) - 1 + side
        dst = 7 if k == 4 else 2 * k - 1 + side
        to = (z + 1) % 8 if side == 0 else (z + 7) % 8
        return remote(wts.at[src, pl.ds(at, n)], wts.at[dst, pl.ds(at, n)],
                      w_send.at[side, k - 1, ch], w_recv.at[dst, ch], dp_of(x_hi, to, core), tensor)

    w_copy(0, 1, 0).start()
    w_copy(1, 1, 1).start()
    w_copy(0, 1, 1).start()
    w_copy(1, 1, 0).start()
    own_tok = toks.at[0, mine]
    to_other = remote(own_tok, toks.at[0, mine], t_send.at[0], t_recv.at[0], dp_of(x_hi, z, other), tensor)
    to_far = remote(own_tok, toks.at[1, mine], t_send.at[1], t_recv.at[1], dp_of(1 - x_hi, z, core), tensor)
    relay = remote(toks.at[1, mine], toks.at[1, mine], t_send.at[2], t_recv.at[2], dp_of(x_hi, z, other), tensor)
    sq_copy = remote(sq_out, sq_in.at[tensor], s_send.at[0], s_recv.at[tensor], dp, owner)

    @pl.when(owner != tensor)
    def _():
        sq_copy.start()
    to_other.start()
    to_far.start()

    def over_tensor(src, dst, send, recv, act):
        def body(i, carry):
            to = (tensor + i) % 8
            if act == "recv":
                remote(src, dst.at[to], send.at[i], recv.at[to], dp, to).wait_recv()
            elif act == "start":
                remote(src, dst.at[tensor], send.at[i], recv.at[tensor], dp, to).start()
            else:
                remote(src, dst.at[tensor], send.at[i], recv.at[tensor], dp, to).wait_send()
            return carry
        lax.fori_loop(1, 8, body, 0)

    over_tensor(low_out, low_in, l_send, l_recv, "start")

    def zsrc_of(j):
        k = (j + 1) // 2
        return (z + 8 + k - 2 * k * (j % 2)) % 8

    def y_copy(j, g):
        zs = zsrc_of(j)
        return remote(outgoing.at[j, g], arrived.at[y, zs % 2, core], y_send.at[j, g],
                      y_recv.at[y, zs % 2, core], dp_of(x_hi, z, g), x_lo * 4 + zs // 2)

    def local(j, g):
        return jnp.logical_and(zsrc_of(j) // 2 == y, core == g)

    def item(j, g):
        p = lax.dot_general(toks[g], wts[j], (((1,), (1,)), ((), ())), preferred_element_type=F32)
        p = p.T.astype(BF)
        here = local(j, g)

        @pl.when(here)
        def _():
            arrived[y, zsrc_of(j) % 2, core] = p

        @pl.when(jnp.logical_not(here))
        def _():
            outgoing[j, g] = p
            y_copy(j, g).start()

    def items(lo, hi, g):
        def body(j, carry):
            item(j, g)
            return carry
        lax.fori_loop(lo, hi, body, 0)

    def msg_copy(i):
        return remote(msg, msgs.at[dp % 4], m_send.at[i], m_recv.at[dp % 4], (dp + i) % 32, tensor)

    def publish():
        def arrive(i, carry):
            frm = (tensor + i) % 8
            remote(sq_out, sq_in.at[frm], s_send.at[0], s_recv.at[frm], dp, frm).wait_recv()
            return carry
        lax.fori_loop(1, 8, arrive, 0)
        total = sq_in[0]
        for i in range(1, 8):
            total = total + sq_in[i]
        total = total[0:1]
        high = total.astype(BF).astype(F32)
        rest = total - high
        msg_f[:, 0:COLS] = a_ref[...].astype(F32)
        for i in range(3):
            msg_f[i:i + 1, 144:192] = high[:, 48 * i:48 * (i + 1)]
            msg_f[3 + i:4 + i, 144:192] = rest[:, 48 * i:48 * (i + 1)]
        packed = msg_f[...].astype(BF)
        msg[...] = packed
        msgs[dp % 4] = packed

        def send(i, carry):
            msg_copy(i).start()
            return carry
        lax.fori_loop(1, 32, send, 0)

    def receive():
        for j in range(4):
            @pl.when(dp != tensor * 4 + j)
            def _():
                remote(msg, msgs.at[j], m_send.at[0], m_recv.at[j], dp, tensor).wait_recv()
        for j in range(4):
            m = msgs[j].astype(F32)
            a_all[:, COLS * j:COLS * (j + 1)] = m[:, 0:COLS]
            for i in range(3):
                at = COLS * j + 48 * i
                sq_all[:, at:at + 48] = m[i:i + 1, 144:192] + m[3 + i:4 + i, 144:192]

    def norms():
        return jnp.sqrt(sq_all[...] + 1e-6)

    def backward():
        scale = mag_ref[...] / norms()
        d = (cot_ref[...].astype(F32) * scale).astype(BF)
        dpre[...] = d
        back = lax.dot_general(a_all[...].astype(BF), d, (((1,), (1,)), ((), ())), preferred_element_type=F32)
        back_out[...] = back
        back_in[tensor] = back
        over_tensor(back_out, back_in, b_send, b_recv, "start")

    group = x_hi * 2 + core

    def spread_copy(i):
        to = (group + i) % 4
        return remote(spread.at[to], spread_in.at[group], d_send.at[i], d_recv.at[group],
                      dp_of(to // 2, z, to % 2), tensor)

    def gradients():
        over_tensor(low_out, low_in, l_send, l_recv, "recv")
        over_tensor(back_out, back_in, b_send, b_recv, "recv")
        low, back = low_in[0], back_in[0]
        for i in range(1, 8):
            low = low + low_in[i]
            back = back + back_in[i]
        low, back = low.astype(BF), back.astype(BF)
        grad_b = jnp.dot(back, toks[0, mine], preferred_element_type=F32)
        grad_a = jnp.dot(low, dpre[...], preferred_element_type=F32)
        for x in range(2):
            for zz in range(8):
                for c in range(2):
                    i = x * 16 + zz * 2 + c
                    spread[x * 2 + c, zz, :, 0:72] = grad_b[:, 72 * i:72 * (i + 1)]
                    spread[x * 2 + c, zz, :, 72:90] = grad_a[:, 18 * i:18 * (i + 1)]
        for i in range(1, 4):
            spread_copy(i).start()
        extra[...] = lax.dot_general(low, a_all[...].astype(BF), (((0,), (0,)), ((), ())),
                                     preferred_element_type=F32)

    def plane_copy(i):
        to = (z + i) % 8
        return remote(plane.at[to], plane_in.at[z], p_send.at[i], p_recv.at[z], dp_of(x_hi, to, core), tensor)

    def sum_plane():
        total = spread[group]
        for i in range(1, 4):
            frm = (group + i) % 4
            remote(spread.at[0], spread_in.at[frm], d_send.at[0], d_recv.at[frm], dp, tensor).wait_recv()
            total = total + spread_in[frm]
        plane[...] = total

        def send(i, carry):
            plane_copy(i).start()
            return carry
        lax.fori_loop(1, 8, send, 0)

    def sum_planes():
        total = plane[z]
        for i in range(1, 8):
            frm = (z + i) % 8
            remote(plane.at[0], plane_in.at[frm], p_send.at[0], p_recv.at[frm], dp, tensor).wait_recv()
            total = total + plane_in[frm]
        grads_ref[...] = total

    def ring(k, first):
        for side in (0, 1):
            ch = first if side == 0 else 1 - first
            w_copy(side, k, ch).wait_recv()
            if k < 3 or first == 0:
                w_copy(side, k + 1, ch).start()

    to_other.wait_recv()
    items(0, 1, 0)
    pl.when(owner == tensor)(publish)
    ring(1, 0)
    receive()
    backward()
    ring(1, 1)
    items(1, 3, 0)
    gradients()
    ring(2, 0)
    sum_plane()
    ring(2, 1)
    items(3, 5, 0)
    to_far.wait_recv()
    relay.start()
    relay.wait_recv()
    items(0, 5, 1)
    ring(3, 0)
    sum_planes()
    ring(3, 1)
    items(5, 7, 0)
    items(5, 7, 1)
    w_copy(0, 4, 0).wait_recv()
    w_copy(1, 4, 1).wait_recv()
    items(7, 8, 0)
    items(7, 8, 1)

    tok_hi = jnp.where(core == 0, x_hi, 1 - x_hi)

    def x_copy(zp, ct):
        return remote(turned.at[zp, pl.ds(ct * TOK, TOK)], halves.at[x_lo, zp], x_send.at[zp, ct],
                      x_recv.at[x_lo, zp], dp_of(tok_hi, z, ct), x_hi * 4 + y)

    def to_self(ct):
        return jnp.logical_and(jnp.logical_and(tok_hi == x_hi, x_lo == x_hi), core == ct)

    for zp in range(2):
        parts = []
        for cs in range(2):
            for k in range(4):
                ys = (y + k) % 4
                away = jnp.logical_or(k > 0, core != cs)

                def arrive(ys=ys, cs=cs):
                    remote(outgoing.at[0, 0], arrived.at[ys, zp, cs], y_send.at[0, 0], y_recv.at[ys, zp, cs],
                           dp, tensor).wait_recv()
                if k == 0:
                    pl.when(core != cs)(arrive)
                else:
                    arrive()
            total = arrived[0, zp, cs].astype(F32)
            for ys in range(1, 4):
                total = total + arrived[ys, zp, cs].astype(F32)
            parts.append(total)
        both = jnp.concatenate(parts, axis=0).T.astype(BF)
        turned[zp] = both
        for ct in range(2):
            @pl.when(to_self(ct))
            def _():
                halves[x_lo, zp] = both[ct * TOK:(ct + 1) * TOK]

            @pl.when(jnp.logical_not(to_self(ct)))
            def _():
                x_copy(zp, ct).start()

    for zp in range(2):
        for xl in range(2):
            sx_hi = x_lo
            score = jnp.where(sx_hi == x_hi, 0, 1)
            own = jnp.logical_and(jnp.logical_and(sx_hi == x_hi, xl == x_lo), score == core)

            @pl.when(jnp.logical_not(own))
            def _():
                remote(turned.at[0, pl.ds(0, TOK)], halves.at[xl, zp], x_send.at[0, 0], x_recv.at[xl, zp],
                       dp, tensor).wait_recv()
        cols = slice(zp * 288, (zp + 1) * 288)
        extra[:, cols] = extra[:, cols] + (halves[0, zp].astype(F32) + halves[1, zp].astype(F32))
    pre = extra[...]
    norm = norms()
    mag_row = jnp.sum(cot_ref[...].astype(F32) * pre, axis=0, keepdims=True) / norm
    for i in range(32):
        mag_out[i, :, 0:18] = mag_row[:, 18 * i:18 * (i + 1)]

    def mag_copy(i):
        to = (dp + i) % 32
        return remote(mag_out.at[to], mag_in.at[dp], g_send.at[i], g_recv.at[dp], to, tensor)

    def mag_start(i, carry):
        mag_copy(i).start()
        return carry
    lax.fori_loop(1, 32, mag_start, 0)
    mixed_ref[...] = (pre * (mag_ref[...] / norm)).astype(BF)

    for k in (1, 2, 3, 4):
        for side in (0, 1):
            for ch in (0, 1):
                if k < 4 or ch == side:
                    w_copy(side, k, ch).wait_send()
    @pl.when(owner != tensor)
    def _():
        sq_copy.wait_send()

    @pl.when(owner == tensor)
    def _():
        def sent(i, carry):
            msg_copy(i).wait_send()
            return carry
        lax.fori_loop(1, 32, sent, 0)
    over_tensor(low_out, low_in, l_send, l_recv, "send")
    over_tensor(back_out, back_in, b_send, b_recv, "send")
    for i in range(1, 4):
        spread_copy(i).wait_send()

    def plane_sent(i, carry):
        plane_copy(i).wait_send()
        return carry
    lax.fori_loop(1, 8, plane_sent, 0)
    to_other.wait_send()
    to_far.wait_send()
    relay.wait_send()
    def drain(j, carry):
        for g in range(2):
            @pl.when(jnp.logical_not(local(j, g)))
            def _():
                y_copy(j, g).wait_send()
        return carry
    lax.fori_loop(0, 8, drain, 0)
    for zp in range(2):
        for ct in range(2):
            @pl.when(jnp.logical_not(to_self(ct)))
            def _():
                x_copy(zp, ct).wait_send()

    def mag_arrive(i, total):
        frm = (dp + i) % 32
        remote(mag_out.at[0], mag_in.at[frm], g_send.at[0], g_recv.at[frm], dp, tensor).wait_recv()
        return total + mag_in[frm]
    gmag_ref[...] = lax.fori_loop(1, 32, mag_arrive, mag_out[dp])

    def mag_sent(i, carry):
        mag_copy(i).wait_send()
        return carry
    lax.fori_loop(1, 32, mag_sent, 0)


def body(hidden, weight, factor_b, factor_a, magnitude, cotangent):
    any_spec, vmem_spec = pl.BlockSpec(memory_space=pl.ANY), pl.BlockSpec(memory_space=pltpu.VMEM)
    dma, vmem = pltpu.SemaphoreType.DMA, pltpu.VMEM
    mixed, grads, gmag = pl.pallas_call(
        kernel,
        name="dora",
        out_shape=(jax.ShapeDtypeStruct((TOK, OUT), BF), jax.ShapeDtypeStruct((16, 128), F32),
                   jax.ShapeDtypeStruct((1, 128), F32)),
        in_specs=[any_spec, any_spec] + [vmem_spec] * 4,
        out_specs=(vmem_spec,) * 3,
        scratch_shapes=[
            vmem((2, 2 * TOK, HID), BF),
            vmem((8, COLS, HID), BF),
            vmem((8, 2, COLS, 2 * TOK), BF),
            vmem((4, 2, 2, COLS, 2 * TOK), BF),
            vmem((2, 2 * TOK, 288), BF),
            vmem((2, 2, TOK, 288), BF),
            vmem((8, COLS), F32), vmem((8, 8, COLS), F32),
            vmem((16, 256), F32), vmem((16, 256), BF), vmem((4, 16, 256), BF),
            vmem((16, OUT), F32), vmem((1, OUT), F32),
            vmem((8, 16, TOK), F32), vmem((8, 16, TOK), F32), vmem((16, TOK), F32), vmem((16, TOK), F32),
            vmem((TOK, OUT), BF), vmem((TOK, OUT), F32),
            vmem((4, 8, 16, 128), F32), vmem((4, 8, 16, 128), F32),
            vmem((8, 16, 128), F32), vmem((8, 16, 128), F32),
            vmem((32, 1, 128), F32), vmem((32, 1, 128), F32),
            dma((2,)), dma((2, 4, 2)), dma((8, 2)), dma((3,)), dma((3,)),
            dma((8, 2)), dma((4, 2, 2)), dma((2, 2)), dma((2, 2)),
            dma((1,)), dma((8,)), dma((32,)), dma((4,)), dma((8,)), dma((8,)), dma((8,)), dma((8,)),
            dma((4,)), dma((4,)), dma((8,)), dma((8,)), dma((32,)), dma((32,)),
        ],
        compiler_params=pltpu.CompilerParams(
            collective_id=0, has_side_effects=True, vmem_limit_bytes=48 * 1024 * 1024
        ),
    )(hidden, weight.T, factor_b.T, factor_a, magnitude.reshape(1, OUT), cotangent)
    return mixed, gmag[0, :18], grads[:, 72:90], grads[:, :72].T


def solution(mesh):
    return jax.shard_map(
        body,
        mesh=mesh,
        in_specs=(
            P("dp", "tensor"),
            P("tensor", "dp"),
            P("tensor", None),
            P(None, "dp"),
            P("tensor"),
            P("dp", "tensor"),
        ),
        out_specs=(
            P("dp", "tensor"),
            P(("tensor", "dp")),
            P(None, ("tensor", "dp")),
            P(("tensor", "dp"), None),
        ),
        check_vma=False,
    )
```

time: 210 us -> 146 us (0.70)
  blocking collectives: 69.7 us -> 0 us
  Pallas kernels: 72.6 us -> 137 us
  starting transfers between devices: 46.7 us -> 0 us
  matrix products: 6.01 us -> 0 us
  waiting for transfers between devices: 4.9 us -> 0 us
    pallas_call x1, Pallas kernels: 72.6 us -> 137 us  [body(): pl.pallas_call(kernel, name='dora', out_shape=(jax.ShapeDtypeStruct((TOK,...]
    all_to_all x2 -> x0, starting transfers between devices: 46.7 us -> none  [copy_for_each(): return lax.all_to_all(copies, axis, split_axis=0, concat_axis=0, tiled=True)]
    all_gather x1 -> x0, blocking collectives: 42.6 us -> none  [body(): full_a = lax.all_gather(lowrank_factor_a, 'dp', axis=1, tiled=True)]
    all_to_all x2 -> x0, blocking collectives: 27 us -> none  [the longest x1 15.6 us: summed_on_arrival(): lax.all_to_all(pieces, axis, split_axis=0, concat_axis=0, tiled=True)]
    dot_general x6 -> x0, matrix products: 6.01 us -> none  [the longest x1 1.93 us: body(): jnp.dot(lowrank_block_update, own_a, preferred_element_type=jnp.float32)]
    all_to_all x2 -> x0, waiting for transfers between devices: 4.9 us -> none  [copy_for_each(): return lax.all_to_all(copies, axis, split_axis=0, concat_axis=0, tiled=True)]
    unnamed x14 -> x11, local copies, waits for them, and re-layouts: 2.54 us -> 5.79 us
  transfers between devices with their start and end apart: 2 -> 0, of which waited for: 1 -> 0; matrix products, arithmetic and copies ran while one was open for 1% -> 0% of each run, Pallas kernels for 35% -> 0%
where the time goes in v2:
time: 146 us
  Pallas kernels  137 us (94%)
  local copies, waits for them, and re-layouts  8.27 us (6%)
    pallas_call x1, Pallas kernels, body(): pl.pallas_call(kernel, name='dora', out_shape=(jax.ShapeDtypeStruct((TOK,...  137 us
    unnamed x11, local copies, waits for them, and re-layouts  5.79 us

profile of v2, /device:TPU:1, one launch (start us, length us, event | category | flops | bytes accessed | tf_op | source)
XLA Modules:
  0.0 145.9 jit_solution(6974017026031120654)
XLA Ops:
  0.6 0.7 reshape.11.mag_ref
  1.3 0.0 copy-start
  1.3 1.4 copy-done
  2.7 0.0 copy-start.1
  2.7 1.1 copy-done.1
  3.8 0.0 copy-start.2
  3.8 1.0 copy-done.2
  4.8 0.0 copy-start.3
  4.8 0.9 copy-done.3
  5.7 0.0 copy-start.4
  5.7 0.7 copy-done.4
  6.4 137.0 %dora.1 = (bf16[320,576]{1,0:T(8,128)(2,1)S(1)}, f32[16,128]{1,0:T(8,128)S(1)}, f32[1,128]{1,0:T(1,128)S(1)}) custom-call(bf16[320,2304]{1,0:T(8,128)(2,1)S(1)} %copy-done, bf16[144,2304]{1,0:T(8,128)(2,1)S(1)} %bitcast.6, bf16[16,2304]{1,0:T(8,128)(2,1)S(1)} %bitcast.7, bf16[16,144]{1,0:T(8,128)(2,1)S(1)} %copy-done.4, f32[1,576]{1,0:T(1,128)S(1)} %reshape.11.mag_ref, ...), custom_call_target="tpu_custom_call" | custom-call | tf_op jit(solution)/shard_map/dora/pallas_call | solution.py:424
  143.4 0.5 slice_bitcast_fusion.1
  143.9 0.6 slice_bitcast_fusion
  144.5 0.7 slice.10
  145.2 0.8 copy.11
Async XLA Ops:
  1.3 1.4 copy-start
  2.7 1.1 copy-start.1
  3.8 1.0 copy-start.2
  4.8 0.9 copy-start.3
  5.7 0.7 copy-start.4

commit v3 on v2

v3 whole, which is shorter than its diff:
```python
import functools

import jax
import jax.numpy as jnp
from jax import lax
from jax.experimental import pallas as pl
from jax.experimental.pallas import tpu as pltpu
from jax.sharding import PartitionSpec as P

TOK, HID, COLS, OUT, HALF = 320, 2304, 144, 576, 288
MESH = pl.DeviceIdType.MESH
F32, BF = jnp.float32, jnp.bfloat16
CHUNKS = ((0, 80), (80, 64))
FIRST, LAST = 192, 128
PARTS = ((0, 2 * FIRST), (2 * FIRST, 2 * LAST))


def remote(src, dst, send, recv, dp, tensor):
    return pltpu.make_async_remote_copy(
        src_ref=src, dst_ref=dst, send_sem=send, recv_sem=recv,
        device_id=(dp, tensor), device_id_type=MESH,
    )


def kernel(h_ref, w_ref, b_hbm, a_hbm, mag_hbm, cot_hbm, mixed_ref, grads_ref, gmag_ref,
           b_ref, a_ref, mag_ref, cot_ref, own, toks, wts, outgoing, arrived, turned, halves,
           sq_out, sq_in, msg_f, msg, msgs, a_all, sq_all, norms, scales, low_in, back_in, low_out, back_out,
           dpre, extra, cots,
           spread, spread_in, plane, plane_in, mag_out, mag_in, sums, results,
           loc_sem, w_send, w_recv, t_send, t_recv, y_send, y_recv, x_send, x_recv,
           s_send, s_recv, m_send, m_recv, l_send, l_recv, b_send, b_recv, d_send, d_recv, p_send, p_recv,
           g_send, g_recv):
    dp, tensor = lax.axis_index("dp"), lax.axis_index("tensor")
    x_hi, z, core = dp // 16, (dp // 2) % 8, dp % 2
    x_lo, y = tensor // 4, tensor % 4
    other = 1 - core

    def dp_of(a, b, c):
        return a * 16 + b * 2 + c

    def rows(part, of):
        if part == 0:
            return pl.ds(of * FIRST, FIRST), pl.ds(0, FIRST)
        return pl.ds(2 * FIRST + of * LAST, LAST), pl.ds(FIRST, LAST)

    load_h = pltpu.make_async_copy(h_ref, own, loc_sem.at[0])
    place = []
    for part in range(2):
        there, here = rows(part, core)
        place.append(pltpu.make_async_copy(h_ref.at[here], toks.at[0, there], loc_sem.at[6 + part]))
    load_w = pltpu.make_async_copy(w_ref, wts.at[0], loc_sem.at[1])
    loads = [pltpu.make_async_copy(src, dst, loc_sem.at[2 + i]) for i, (src, dst) in enumerate(
        ((a_hbm, a_ref), (b_hbm, b_ref), (mag_hbm, mag_ref), (cot_hbm, cot_ref)))]
    load_w.start()
    loads[0].start()
    loads[1].start()
    load_h.start()
    place[0].start()
    place[1].start()
    loads[2].start()
    loads[3].start()

    barrier = pltpu.get_barrier_semaphore()

    def greet(p):
        pl.semaphore_signal(barrier, inc=1, device_id=p, device_id_type=MESH)

    near = []
    for k in range(1, 4):
        near.append((dp_of(x_hi, z, core), x_lo * 4 + (y + k) % 4))
        near.append((dp_of(x_hi, z, other), x_lo * 4 + (y + k) % 4))
    for k in range(4):
        near.append((dp, (1 - x_lo) * 4 + (y + k) % 4))
    near.append((dp_of(x_hi, z, other), (1 - x_lo) * 4 + y))
    for c in range(2):
        near.append((dp_of(1 - x_hi, z, c), (1 - x_lo) * 4 + y))
    for p in near:
        greet(p)

    def greet_dp(i, carry):
        greet(((dp + i) % 32, tensor))
        return carry
    lax.fori_loop(1, 32, greet_dp, 0)

    owner = dp // 4
    load_w.wait()
    loads[0].wait()
    loads[1].wait()
    merged = wts[0].astype(F32) + lax.dot_general(
        a_ref[...], b_ref[...], (((0,), (0,)), ((), ())), preferred_element_type=F32)
    squares = merged * merged
    lanes = squares[:, 0:128]
    for i in range(1, 18):
        lanes = lanes + squares[:, 128 * i:128 * (i + 1)]
    own_sq = jnp.sum(lanes.T, axis=0, keepdims=True)
    sq_row = jnp.broadcast_to(own_sq, (8, COLS))

    @pl.when(owner == tensor)
    def _():
        sq_in[tensor] = sq_row

    @pl.when(owner != tensor)
    def _():
        sq_out[...] = sq_row

    load_h.wait()
    low_part = lax.dot_general(b_ref[...], own[...], (((1,), (1,)), ((), ())), preferred_element_type=F32)
    low_out[...] = low_part
    low_in[tensor] = low_part
    spread[...] = jnp.zeros_like(spread)
    msg_f[...] = jnp.zeros_like(msg_f)

    loads[2].wait()
    loads[3].wait()
    with jax.named_scope('barrier_wait'):
        pl.semaphore_wait(barrier, len(near) + 31)

    def w_copy(side, k, ch):
        at, n = CHUNKS[ch]
        src = 0 if k == 1 else 2 * (k - 1) - 1 + side
        dst = 7 if k == 4 else 2 * k - 1 + side
        to = (z + 1) % 8 if side == 0 else (z + 7) % 8
        return remote(wts.at[src, pl.ds(at, n)], wts.at[dst, pl.ds(at, n)],
                      w_send.at[side, k - 1, ch], w_recv.at[dst, ch], dp_of(x_hi, to, core), tensor)

    w_copy(0, 1, 0).start()
    w_copy(1, 1, 1).start()
    w_copy(0, 1, 1).start()
    w_copy(1, 1, 0).start()
    to_other, to_far, relay = [], [], []
    for part in range(2):
        there, here = rows(part, core)
        to_other.append(remote(own.at[here], toks.at[0, there], t_send.at[0, part], t_recv.at[0, part],
                               dp_of(x_hi, z, other), tensor))
        to_far.append(remote(own.at[here], toks.at[1, there], t_send.at[1, part], t_recv.at[1, part],
                             dp_of(1 - x_hi, z, core), tensor))
        relay.append(remote(toks.at[1, there], toks.at[1, there], t_send.at[2, part], t_recv.at[2, part],
                            dp_of(x_hi, z, other), tensor))

    sq_copy = remote(sq_out, sq_in.at[tensor], s_send.at[0], s_recv.at[tensor], dp, owner)

    @pl.when(owner != tensor)
    def _():
        sq_copy.start()

    def over_tensor(src, dst, send, recv, act):
        def body(i, carry):
            to = (tensor + i) % 8
            if act == "recv":
                remote(src, dst.at[to], send.at[i], recv.at[to], dp, to).wait_recv()
            elif act == "start":
                remote(src, dst.at[tensor], send.at[i], recv.at[tensor], dp, to).start()
            else:
                remote(src, dst.at[tensor], send.at[i], recv.at[tensor], dp, to).wait_send()
            return carry
        lax.fori_loop(1, 8, body, 0)

    to_other[0].start()
    to_other[1].start()
    over_tensor(low_out, low_in, l_send, l_recv, "start")
    to_far[0].start()
    to_far[1].start()

    def zsrc_of(j):
        k = (j + 1) // 2
        return (z + 8 + k - 2 * k * (j % 2)) % 8

    def summer(j, g):
        return (zsrc_of(j) + 2 * g + core) % 4

    def y_copy(j, g, part):
        lanes = pl.ds(*PARTS[part])
        return remote(outgoing.at[j, g, :, lanes], arrived.at[j, y, :, lanes], y_send.at[j, g, part],
                      y_recv.at[j, y, part], dp, x_lo * 4 + summer(j, g))

    def local(j, g):
        return summer(j, g) == y

    def item(j, g, parts=(0, 1)):
        lo, hi = PARTS[parts[0]][0], sum(PARTS[parts[-1]])
        p = lax.dot_general(toks[g, lo:hi], wts[j], (((1,), (1,)), ((), ())), preferred_element_type=F32)
        p = p.T.astype(BF)
        here = local(j, g)

        @pl.when(here)
        def _():
            arrived[j, y, :, lo:hi] = p

        @pl.when(jnp.logical_not(here))
        def _():
            outgoing[j, g, :, lo:hi] = p
            for part in parts:
                y_copy(j, g, part).start()

    def items(lo, hi, g, parts=(0, 1)):
        def body(j, carry):
            item(j, g, parts)
            return carry
        lax.fori_loop(lo, hi, body, 0)

    def items_both(lo, hi):
        def body(i, carry):
            item(lo + i // 2, i % 2)
            return carry
        lax.fori_loop(0, 2 * (hi - lo), body, 0)

    def msg_copy(i):
        return remote(msg, msgs.at[dp % 4], m_send.at[i], m_recv.at[dp % 4], (dp + i) % 32, tensor)

    def publish():
        def arrive(i, carry):
            frm = (tensor + i) % 8
            remote(sq_out, sq_in.at[frm], s_send.at[0], s_recv.at[frm], dp, frm).wait_recv()
            return carry
        lax.fori_loop(1, 8, arrive, 0)
        total = sq_in[0]
        for i in range(1, 8):
            total = total + sq_in[i]
        total = total[0:1]
        high = total.astype(BF).astype(F32)
        rest = total - high
        msg_f[:, 0:COLS] = a_ref[...].astype(F32)
        for i in range(3):
            msg_f[i:i + 1, 144:192] = high[:, 48 * i:48 * (i + 1)]
            msg_f[3 + i:4 + i, 144:192] = rest[:, 48 * i:48 * (i + 1)]
        packed = msg_f[...].astype(BF)
        msg[...] = packed
        msgs[dp % 4] = packed

        def send(i, carry):
            msg_copy(i).start()
            return carry
        lax.fori_loop(1, 32, send, 0)

    def receive():
        for j in range(4):
            @pl.when(dp != tensor * 4 + j)
            def _():
                remote(msg, msgs.at[j], m_send.at[0], m_recv.at[j], dp, tensor).wait_recv()
        for j in range(4):
            m = msgs[j].astype(F32)
            zp, at = j // 2, COLS * (j % 2)
            a_all[zp, :, at:at + COLS] = m[:, 0:COLS]
            for i in range(3):
                sq_all[zp, :, at + 48 * i:at + 48 * (i + 1)] = m[i:i + 1, 144:192] + m[3 + i:4 + i, 144:192]

    def backward():
        back = None
        mags = mag_ref[...].reshape(1, OUT)
        for zp in range(2):
            norm = jnp.sqrt(sq_all[zp] + 1e-6)
            scale = mags[:, HALF * zp:HALF * (zp + 1)] / norm
            norms[zp] = norm
            scales[zp] = scale
            cot = cot_ref[:, HALF * zp:HALF * (zp + 1)].astype(F32)
            cots[zp] = cot
            d = (cot * scale).astype(BF)
            dpre[zp] = d
            part = lax.dot_general(a_all[zp].astype(BF), d, (((1,), (1,)), ((), ())), preferred_element_type=F32)
            back = part if back is None else back + part
        back_out[...] = back
        back_in[tensor] = back
        over_tensor(back_out, back_in, b_send, b_recv, "start")

    group = x_hi * 2 + core

    def spread_copy(i):
        to = (group + i) % 4
        return remote(spread.at[to], spread_in.at[group], d_send.at[i], d_recv.at[group],
                      dp_of(to // 2, z, to % 2), tensor)

    def gradients():
        over_tensor(low_out, low_in, l_send, l_recv, "recv")
        over_tensor(back_out, back_in, b_send, b_recv, "recv")
        low, back = low_in[0], back_in[0]
        for i in range(1, 8):
            low = low + low_in[i]
            back = back + back_in[i]
        low, back = low.astype(BF), back.astype(BF)
        grad_b = jnp.dot(back, own[...], preferred_element_type=F32)
        grad_a = [jnp.dot(low, dpre[zp], preferred_element_type=F32) for zp in range(2)]
        for x in range(2):
            for zz in range(8):
                for c in range(2):
                    i = x * 16 + zz * 2 + c
                    spread[x * 2 + c, zz, :, 0:72] = grad_b[:, 72 * i:72 * (i + 1)]
                    spread[x * 2 + c, zz, :, 72:90] = grad_a[x][:, 18 * (i % 16):18 * (i % 16 + 1)]
        for i in range(1, 4):
            spread_copy(i).start()
        for zp in range(2):
            extra[zp] = lax.dot_general(low, a_all[zp].astype(BF), (((0,), (0,)), ((), ())),
                                        preferred_element_type=F32)

    def plane_copy(i):
        to = (z + i) % 8
        return remote(plane.at[to], plane_in.at[z], p_send.at[i], p_recv.at[z], dp_of(x_hi, to, core), tensor)

    def sum_plane():
        total = spread[group]
        for i in range(1, 4):
            frm = (group + i) % 4
            remote(spread.at[0], spread_in.at[frm], d_send.at[0], d_recv.at[frm], dp, tensor).wait_recv()
            total = total + spread_in[frm]
        plane[...] = total

        def send(i, carry):
            plane_copy(i).start()
            return carry
        lax.fori_loop(1, 8, send, 0)

    def sum_planes():
        total = plane[z]
        for i in range(1, 8):
            frm = (z + i) % 8
            remote(plane.at[0], plane_in.at[frm], p_send.at[0], p_recv.at[frm], dp, tensor).wait_recv()
            total = total + plane_in[frm]
        grads_ref[...] = total

    def ring(k, first):
        for side in (0, 1):
            ch = first if side == 0 else 1 - first
            w_copy(side, k, ch).wait_recv()
            if k < 3 or first == 0:
                w_copy(side, k + 1, ch).start()

    def x_copy(j, g, ct):
        zs = zsrc_of(j)
        tok_hi = jnp.where(g == 0, x_hi, 1 - x_hi)
        return remote(turned.at[j, ct], halves.at[x_lo, zs % 2, core], x_send.at[j, ct],
                      x_recv.at[x_lo, zs % 2, core], dp_of(tok_hi, z, ct), x_hi * 4 + zs // 2)

    def to_self(j, g, ct):
        same = jnp.logical_and(g == 0, x_lo == x_hi)
        return jnp.logical_and(same, jnp.logical_and(zsrc_of(j) // 2 == y, core == ct))

    def active(j, g):
        return summer(j, g) == y

    def stage_two(j, g):
        for k in range(1, 4):
            ys = (y + k) % 4
            for part in range(2):
                lanes = pl.ds(*PARTS[part])
                remote(outgoing.at[0, 0, :, lanes], arrived.at[j, ys, :, lanes], y_send.at[0, 0, part],
                       y_recv.at[j, ys, part], dp, tensor).wait_recv()
        total = arrived[j, 0].astype(F32)
        for ys in range(1, 4):
            total = total + arrived[j, ys].astype(F32)
        total = total.astype(BF)
        for ct in range(2):
            part = jnp.concatenate(
                [total[:, ct * FIRST:(ct + 1) * FIRST],
                 total[:, 2 * FIRST + ct * LAST:2 * FIRST + (ct + 1) * LAST]], axis=1)
            mine_too = to_self(j, g, ct)

            @pl.when(mine_too)
            def _():
                halves[x_lo, zsrc_of(j) % 2, core] = part

            @pl.when(jnp.logical_not(mine_too))
            def _():
                turned[j, ct] = part
                x_copy(j, g, ct).start()

    def second(lo, hi, g):
        def unit(j, carry):
            pl.when(active(j, g))(lambda: stage_two(j, g))
            return carry
        lax.fori_loop(lo, hi, unit, 0)

    def steps_of(zp):
        away = (2 * y + zp - z + 8) % 8
        return jnp.where(away > 4, 8 - away, away)

    with jax.named_scope("a0"):
        for part in range(2):
            place[part].wait()
            to_other[part].wait_recv()
    items(0, 1, 0)
    with jax.named_scope("a1_publish"):
        pl.when(owner == tensor)(publish)
    with jax.named_scope("a2_ring10"):
        ring(1, 0)
    with jax.named_scope("a3_ring11"):
        ring(1, 1)
    items(1, 3, 0)
    with jax.named_scope("a4_far0"):
        to_far[0].wait_recv()
    relay[0].start()
    with jax.named_scope("a5_ring20"):
        ring(2, 0)
    with jax.named_scope("a6_relay0"):
        relay[0].wait_recv()
    items(0, 3, 1, (0,))
    with jax.named_scope("a7_receive"):
        receive()
    backward()
    with jax.named_scope("a8_ring21"):
        ring(2, 1)
    items(3, 5, 0)
    items(3, 5, 1, (0,))
    with jax.named_scope("a9_far1"):
        to_far[1].wait_recv()
    relay[1].start()
    second(0, 3, 0)
    with jax.named_scope("aa_relay1"):
        relay[1].wait_recv()
    items(0, 5, 1, (1,))
    with jax.named_scope("ab_ring30"):
        ring(3, 0)
    with jax.named_scope("b0_grads"):
        gradients()
    with jax.named_scope("b1_ring31"):
        ring(3, 1)
    with jax.named_scope("b2_items"):
        items_both(5, 7)
    with jax.named_scope("b3_plane"):
        sum_plane()
    with jax.named_scope("b4_second"):
        second(3, 5, 0)
    with jax.named_scope("b5_last"):
        w_copy(0, 4, 0).wait_recv()
        w_copy(1, 4, 1).wait_recv()
    with jax.named_scope("b6_items"):
        items_both(7, 8)
    with jax.named_scope("b8_second"):
        second(0, 5, 1)
    with jax.named_scope("b9_second"):
        second(5, 7, 0)
        second(5, 7, 1)
    with jax.named_scope("ba_second"):
        second(7, 8, 0)
        second(7, 8, 1)

    def finish(i, carry):
        zp = jnp.where(steps_of(0) <= steps_of(1), i, 1 - i)
        parts = []
        for cs in range(2):
            for xl in range(2):
                far = jnp.where(x_lo == x_hi, 0, 1)
                frm = (2 * y + zp + 2 * far + cs) % 4
                own = jnp.logical_and(jnp.logical_and(x_lo == x_hi, xl == x_lo),
                                      jnp.logical_and(frm == y, core == cs))

                @pl.when(jnp.logical_not(own))
                def _():
                    remote(turned.at[0, 0], halves.at[xl, zp, cs], x_send.at[0, 0], x_recv.at[xl, zp, cs],
                           dp, tensor).wait_recv()
            parts.append(halves[0, zp, cs].astype(F32) + halves[1, zp, cs].astype(F32))
        pre = extra[zp] + jnp.concatenate(parts, axis=0).T
        sums[zp] = jnp.sum(cots[zp] * pre, axis=0, keepdims=True) / norms[zp]
        results[zp] = pre * scales[zp]
        return carry
    with jax.named_scope("c0_finish"):
        lax.fori_loop(0, 2, finish, 0)
    for i in range(32):
        mag_out[i, :, 0:18] = sums[i // 16][:, 18 * (i % 16):18 * (i % 16 + 1)]

    def mag_copy(i):
        to = (dp + i) % 32
        return remote(mag_out.at[to], mag_in.at[dp], g_send.at[i], g_recv.at[dp], to, tensor)

    def mag_start(i, carry):
        mag_copy(i).start()
        return carry
    with jax.named_scope("c1_mag"):
        lax.fori_loop(1, 32, mag_start, 0)
    with jax.named_scope("b7_planes"):
        sum_planes()
    with jax.named_scope("c2_mixed"):
        for zp in range(2):
            mixed_ref[:, HALF * zp:HALF * (zp + 1)] = results[zp].astype(BF)

    for k in (1, 2, 3, 4):
        for side in (0, 1):
            for ch in (0, 1):
                if k < 4 or ch == side:
                    w_copy(side, k, ch).wait_send()
    @pl.when(owner != tensor)
    def _():
        sq_copy.wait_send()

    @pl.when(owner == tensor)
    def _():
        def sent(i, carry):
            msg_copy(i).wait_send()
            return carry
        lax.fori_loop(1, 32, sent, 0)
    over_tensor(low_out, low_in, l_send, l_recv, "send")
    over_tensor(back_out, back_in, b_send, b_recv, "send")
    for i in range(1, 4):
        spread_copy(i).wait_send()

    def plane_sent(i, carry):
        plane_copy(i).wait_send()
        return carry
    lax.fori_loop(1, 8, plane_sent, 0)
    for copies in (to_other, to_far, relay):
        for part in range(2):
            copies[part].wait_send()
    def drain(j, carry):
        for g in range(2):
            @pl.when(jnp.logical_not(local(j, g)))
            def _():
                for part in range(2):
                    y_copy(j, g, part).wait_send()
        return carry
    lax.fori_loop(0, 8, drain, 0)

    def drain_two(j, carry):
        for g in range(2):
            for ct in range(2):
                @pl.when(jnp.logical_and(active(j, g), jnp.logical_not(to_self(j, g, ct))))
                def _():
                    x_copy(j, g, ct).wait_send()
        return carry
    lax.fori_loop(0, 8, drain_two, 0)

    def mag_arrive(i, total):
        frm = (dp + i) % 32
        remote(mag_out.at[0], mag_in.at[frm], g_send.at[0], g_recv.at[frm], dp, tensor).wait_recv()
        return total + mag_in[frm]
    with jax.named_scope("c3_gmag"):
        gmag_ref[...] = lax.fori_loop(1, 32, mag_arrive, mag_out[dp])

    def mag_sent(i, carry):
        mag_copy(i).wait_send()
        return carry
    lax.fori_loop(1, 32, mag_sent, 0)


def body(hidden, weight, factor_b, factor_a, magnitude, cotangent):
    any_spec, vmem_spec = pl.BlockSpec(memory_space=pl.ANY), pl.BlockSpec(memory_space=pltpu.VMEM)
    dma, vmem = pltpu.SemaphoreType.DMA, pltpu.VMEM
    mixed, grads, gmag = pl.pallas_call(
        kernel,
        name="dora",
        out_shape=(jax.ShapeDtypeStruct((TOK, OUT), BF), jax.ShapeDtypeStruct((16, 128), F32),
                   jax.ShapeDtypeStruct((1, 128), F32)),
        in_specs=[any_spec] * 6,
        out_specs=(vmem_spec,) * 3,
        scratch_shapes=[
            vmem((16, HID), BF), vmem((16, COLS), BF), vmem((OUT,), F32), vmem((TOK, OUT), BF), vmem((TOK, HID), BF),
            vmem((2, 2 * TOK, HID), BF),
            vmem((8, COLS, HID), BF),
            vmem((8, 2, COLS, 2 * TOK), BF),
            vmem((8, 4, COLS, 2 * TOK), BF),
            vmem((8, 2, COLS, TOK), BF),
            vmem((2, 2, 2, COLS, TOK), BF),
            vmem((8, COLS), F32), vmem((8, 8, COLS), F32),
            vmem((16, 256), F32), vmem((16, 256), BF), vmem((4, 16, 256), BF),
            vmem((2, 16, HALF), F32), vmem((2, 1, HALF), F32), vmem((2, 1, HALF), F32), vmem((2, 1, HALF), F32),
            vmem((8, 16, TOK), F32), vmem((8, 16, TOK), F32), vmem((16, TOK), F32), vmem((16, TOK), F32),
            vmem((2, TOK, HALF), BF), vmem((2, TOK, HALF), F32), vmem((2, TOK, HALF), F32),
            vmem((4, 8, 16, 128), F32), vmem((4, 8, 16, 128), F32),
            vmem((8, 16, 128), F32), vmem((8, 16, 128), F32),
            vmem((32, 1, 128), F32), vmem((32, 1, 128), F32), vmem((2, 1, HALF), F32), vmem((2, TOK, HALF), F32),
            dma((8,)), dma((2, 4, 2)), dma((8, 2)), dma((3, 2)), dma((3, 2)),
            dma((8, 2, 2)), dma((8, 4, 2)), dma((8, 2)), dma((2, 2, 2)),
            dma((1,)), dma((8,)), dma((32,)), dma((4,)), dma((8,)), dma((8,)), dma((8,)), dma((8,)),
            dma((4,)), dma((4,)), dma((8,)), dma((8,)), dma((32,)), dma((32,)),
        ],
        compiler_params=pltpu.CompilerParams(
            collective_id=0, has_side_effects=True, vmem_limit_bytes=48 * 1024 * 1024
        ),
    )(hidden, weight.T, factor_b.T, factor_a, magnitude, cotangent)
    return mixed, gmag[0, :18], grads[:, 72:90], grads[:, :72].T


def solution(mesh):
    return jax.shard_map(
        body,
        mesh=mesh,
        in_specs=(
            P("dp", "tensor"),
            P("tensor", "dp"),
            P("tensor", None),
            P(None, "dp"),
            P("tensor"),
            P("dp", "tensor"),
        ),
        out_specs=(
            P("dp", "tensor"),
            P(("tensor", "dp")),
            P(None, ("tensor", "dp")),
            P(("tensor", "dp"), None),
        ),
        check_vma=False,
    )
```

time: 146 us -> 114 us (0.78)
  Pallas kernels: 137 us -> 105 us
    pallas_call x1, Pallas kernels: 137 us -> 105 us  [body(): pl.pallas_call(kernel, name='dora', out_shape=(jax.ShapeDtypeStruct((TOK,...]
    unnamed x11 -> x13, local copies, waits for them, and re-layouts: 5.79 us -> 6.47 us
where the time goes in v3:
time: 114 us
  Pallas kernels  105 us (92%)
  local copies, waits for them, and re-layouts  8.26 us (7%)
    pallas_call x1, Pallas kernels, body(): pl.pallas_call(kernel, name='dora', out_shape=(jax.ShapeDtypeStruct((TOK,...  105 us
    unnamed x13, local copies, waits for them, and re-layouts  6.47 us

profile of v3, /device:TPU:1, one launch (start us, length us, event | category | flops | bytes accessed | tf_op | source)
XLA Modules:
  0.0 113.7 jit_solution(3541878256559612985)
XLA Ops:
  0.6 0.0 copy-start
  0.6 1.4 %copy-done = bf16[320,2304]{1,0:T(8,128)(2,1)S(1)} copy-done((bf16[320,2304]{1,0:T(8,128)(2,1)S(1)}, bf16[320,2304]{1,0:T(8,128)(2,1)}, u32[]{:S(2)}) %copy-start) | copy-done | bytes 1474584
  2.0 0.0 copy-start.1
  2.0 1.1 copy-done.1
  3.1 0.0 copy-start.2
  3.1 1.0 copy-done.2
  4.1 0.0 copy-start.3
  4.1 0.9 copy-done.3
  5.0 0.0 copy-start.4
  5.0 0.7 copy-done.4
  5.7 0.0 copy-start.5
  5.7 0.7 copy-done.5
  6.4 104.8 %dora.1 = (bf16[320,576]{1,0:T(8,128)(2,1)S(1)}, f32[16,128]{1,0:T(8,128)S(1)}, f32[1,128]{1,0:T(1,128)S(1)}) custom-call(bf16[320,2304]{1,0:T(8,128)(2,1)S(1)} %copy-done, bf16[144,2304]{1,0:T(8,128)(2,1)S(1)} %bitcast.6, bf16[16,2304]{1,0:T(8,128)(2,1)S(1)} %bitcast.7, bf16[16,144]{1,0:T(8,128)(2,1)S(1)} %copy-done.4, f32[576]{0:T(1024)S(1)} %copy-done.5, ...), custom_call_target="tpu_custom_call" | custom-call | tf_op jit(solution)/shard_map/dora/pallas_call | solution.py:535
  111.1 0.5 slice_bitcast_fusion.1
  111.7 0.6 slice_bitcast_fusion
  112.3 0.7 slice.10
  112.9 0.8 copy.11
Async XLA Ops:
  0.6 1.4 %copy-start = (bf16[320,2304]{1,0:T(8,128)(2,1)S(1)}, bf16[320,2304]{1,0:T(8,128)(2,1)}, u32[]{:S(2)}) copy-start(bf16[320,2304]{1,0:T(8,128)(2,1)} %h_ref.1) | copy-start | bytes 4423684
  2.0 1.1 copy-start.1
  3.1 1.0 copy-start.2
  4.1 0.9 copy-start.3
  5.0 0.7 copy-start.4
  5.7 0.7 copy-start.5

commit v4 on v3

--- a/solution.py
+++ b/solution.py
@@ -13,6 +13,8 @@
 CHUNKS = ((0, 80), (80, 64))
 FIRST, LAST = 192, 128
 PARTS = ((0, 2 * FIRST), (2 * FIRST, 2 * LAST))
+WHOLE = 5
+FAR = (WHOLE + 1) // 2
 
 
 def remote(src, dst, send, recv, dp, tensor):
@@ -29,7 +31,8 @@
            spread, spread_in, plane, plane_in, mag_out, mag_in, sums, results,
            loc_sem, w_send, w_recv, t_send, t_recv, y_send, y_recv, x_send, x_recv,
            s_send, s_recv, m_send, m_recv, l_send, l_recv, b_send, b_recv, d_send, d_recv, p_send, p_recv,
-           g_send, g_recv):
+           g_send, g_recv,
+           arrived_w, turned_a, turned_b, whole_a, whole_b, flat, e_recv, f_send, f_recv, met):
     dp, tensor = lax.axis_index("dp"), lax.axis_index("tensor")
     x_hi, z, core = dp // 16, (dp // 2) % 8, dp % 2
     x_lo, y = tensor // 4, tensor % 4
@@ -65,55 +68,23 @@
     def greet(p):
         pl.semaphore_signal(barrier, inc=1, device_id=p, device_id_type=MESH)
 
-    near = []
-    for k in range(1, 4):
-        near.append((dp_of(x_hi, z, core), x_lo * 4 + (y + k) % 4))
-        near.append((dp_of(x_hi, z, other), x_lo * 4 + (y + k) % 4))
-    for k in range(4):
-        near.append((dp, (1 - x_lo) * 4 + (y + k) % 4))
-    near.append((dp_of(x_hi, z, other), (1 - x_lo) * 4 + y))
-    for c in range(2):
-        near.append((dp_of(1 - x_hi, z, c), (1 - x_lo) * 4 + y))
+    near = [(dp, (tensor + k) % 8) for k in range(1, 8)]
+    near += [(dp_of(x_hi, (z + 1) % 8, core), tensor), (dp_of(x_hi, (z + 7) % 8, core), tensor),
+             (dp_of(x_hi, z, other), tensor), (dp_of(1 - x_hi, z, core), tensor), (dp_of(1 - x_hi, z, other), tensor)]
     for p in near:
         greet(p)
-
-    def greet_dp(i, carry):
-        greet(((dp + i) % 32, tensor))
-        return carry
-    lax.fori_loop(1, 32, greet_dp, 0)
-
-    owner = dp // 4
-    load_w.wait()
-    loads[0].wait()
-    loads[1].wait()
-    merged = wts[0].astype(F32) + lax.dot_general(
-        a_ref[...], b_ref[...], (((0,), (0,)), ((), ())), preferred_element_type=F32)
-    squares = merged * merged
-    lanes = squares[:, 0:128]
-    for i in range(1, 18):
-        lanes = lanes + squares[:, 128 * i:128 * (i + 1)]
-    own_sq = jnp.sum(lanes.T, axis=0, keepdims=True)
-    sq_row = jnp.broadcast_to(own_sq, (8, COLS))
-
-    @pl.when(owner == tensor)
-    def _():
-        sq_in[tensor] = sq_row
-
-    @pl.when(owner != tensor)
-    def _():
-        sq_out[...] = sq_row
-
-    load_h.wait()
-    low_part = lax.dot_general(b_ref[...], own[...], (((1,), (1,)), ((), ())), preferred_element_type=F32)
-    low_out[...] = low_part
-    low_in[tensor] = low_part
     spread[...] = jnp.zeros_like(spread)
     msg_f[...] = jnp.zeros_like(msg_f)
-
-    loads[2].wait()
-    loads[3].wait()
+    load_w.wait()
+    load_h.wait()
     with jax.named_scope('barrier_wait'):
-        pl.semaphore_wait(barrier, len(near) + 31)
+        pl.semaphore_wait(barrier, len(near))
+
+    def tell(k):
+        for to in ((z + k) % 8, (z + 8 - k) % 8)[:1 if k == 4 else 2]:
+            pl.semaphore_signal(met.at[k // 2], inc=1, device_id=(dp_of(x_hi, to, core), tensor), device_id_type=MESH)
+
+    tell(1)
 
     def w_copy(side, k, ch):
         at, n = CHUNKS[ch]
@@ -137,6 +108,32 @@
         relay.append(remote(toks.at[1, there], toks.at[1, there], t_send.at[2, part], t_recv.at[2, part],
                             dp_of(x_hi, z, other), tensor))
 
+    to_other[0].start()
+    to_other[1].start()
+
+    owner = dp // 4
+    loads[0].wait()
+    loads[1].wait()
+    merged = wts[0].astype(F32) + lax.dot_general(
+        a_ref[...], b_ref[...], (((0,), (0,)), ((), ())), preferred_element_type=F32)
+    squares = merged * merged
+    lanes = squares[:, 0:128]
+    for i in range(1, 18):
+        lanes = lanes + squares[:, 128 * i:128 * (i + 1)]
+    own_sq = jnp.sum(lanes.T, axis=0, keepdims=True)
+    sq_row = jnp.broadcast_to(own_sq, (8, COLS))
+
+    @pl.when(owner == tensor)
+    def _():
+        sq_in[tensor] = sq_row
+
+    @pl.when(owner != tensor)
+    def _():
+        sq_out[...] = sq_row
+
+    low_part = lax.dot_general(b_ref[...], own[...], (((1,), (1,)), ((), ())), preferred_element_type=F32)
+    low_out[...] = low_part
+    low_in[tensor] = low_part
     sq_copy = remote(sq_out, sq_in.at[tensor], s_send.at[0], s_recv.at[tensor], dp, owner)
 
     @pl.when(owner != tensor)
@@ -155,12 +152,15 @@
             return carry
         lax.fori_loop(1, 8, body, 0)
 
-    to_other[0].start()
-    to_other[1].start()
     over_tensor(low_out, low_in, l_send, l_recv, "start")
     to_far[0].start()
     to_far[1].start()
 
+    pl.semaphore_wait(met.at[0], 2)
+    tell(2)
+    loads[2].wait()
+    loads[3].wait()
+
     def zsrc_of(j):
         k = (j + 1) // 2
         return (z + 8 + k - 2 * k * (j % 2)) % 8
@@ -169,22 +169,51 @@
         return (zsrc_of(j) + 2 * g + core) % 4
 
     def y_copy(j, g, part):
-        lanes = pl.ds(*PARTS[part])
-        return remote(outgoing.at[j, g, :, lanes], arrived.at[j, y, :, lanes], y_send.at[j, g, part],
-                      y_recv.at[j, y, part], dp, x_lo * 4 + summer(j, g))
+        zs, lanes = zsrc_of(j), pl.ds(*PARTS[part])
+        return remote(outgoing.at[j, g, :, lanes], arrived.at[zs % 2, y, core, :, lanes], y_send.at[j, g, part],
+                      y_recv.at[zs % 2, y, core, part], dp_of(x_hi, z, g), x_lo * 4 + zs // 2)
+
+    def local_near(j, g):
+        return jnp.logical_and(zsrc_of(j) // 2 == y, core == g)
 
     def local(j, g):
         return summer(j, g) == y
 
-    def item(j, g, parts=(0, 1)):
+    def share_lo(g, part):
+        return (part + g) % 2
+
+    def e_copy(j, g, part):
+        at, n = PARTS[part]
+        return remote(outgoing.at[j, g, :, pl.ds(at, n)], arrived_w.at[j - WHOLE, tensor, :, pl.ds(0, n)],
+                      y_send.at[j, g, part], e_recv.at[j, tensor], dp, share_lo(g, part) * 4 + summer(j, g))
+
+    def local_whole(j, g, part):
+        return jnp.logical_and(local(j, g), share_lo(g, part) == x_lo)
+
+    def item(j, g, parts, whole):
         lo, hi = PARTS[parts[0]][0], sum(PARTS[parts[-1]])
         p = lax.dot_general(toks[g, lo:hi], wts[j], (((1,), (1,)), ((), ())), preferred_element_type=F32)
         p = p.T.astype(BF)
-        here = local(j, g)
+        if whole:
+            for part in parts:
+                at, n = PARTS[part]
+                piece = p[:, at - lo:at - lo + n]
+                here = local_whole(j, g, part)
+
+                @pl.when(here)
+                def _():
+                    arrived_w[j - WHOLE, tensor, :, 0:n] = piece
+
+                @pl.when(jnp.logical_not(here))
+                def _():
+                    outgoing[j, g, :, at:at + n] = piece
+                    e_copy(j, g, part).start()
+            return
+        here = local_near(j, g)
 
         @pl.when(here)
         def _():
-            arrived[j, y, :, lo:hi] = p
+            arrived[zsrc_of(j) % 2, y, core, :, lo:hi] = p
 
         @pl.when(jnp.logical_not(here))
         def _():
@@ -192,17 +221,23 @@
             for part in parts:
                 y_copy(j, g, part).start()
 
+    def split(lo, hi):
+        mid = min(max(lo, WHOLE), hi)
+        return [(a, b, w) for a, b, w in ((lo, mid, False), (mid, hi, True)) if b > a]
+
     def items(lo, hi, g, parts=(0, 1)):
-        def body(j, carry):
-            item(j, g, parts)
-            return carry
-        lax.fori_loop(lo, hi, body, 0)
+        for a, b, whole in split(lo, hi):
+            def body(j, carry, whole=whole):
+                item(j, g, parts, whole)
+                return carry
+            lax.fori_loop(a, b, body, 0)
 
     def items_both(lo, hi):
-        def body(i, carry):
-            item(lo + i // 2, i % 2)
-            return carry
-        lax.fori_loop(0, 2 * (hi - lo), body, 0)
+        for a, b, whole in split(lo, hi):
+            def body(i, carry, a=a, whole=whole):
+                item(a + i // 2, i % 2, (0, 1), whole)
+                return carry
+            lax.fori_loop(0, 2 * (b - a), body, 0)
 
     def msg_copy(i):
         return remote(msg, msgs.at[dp % 4], m_send.at[i], m_recv.at[dp % 4], (dp + i) % 32, tensor)
@@ -323,11 +358,13 @@
             if k < 3 or first == 0:
                 w_copy(side, k + 1, ch).start()
 
-    def x_copy(j, g, ct):
-        zs = zsrc_of(j)
-        tok_hi = jnp.where(g == 0, x_hi, 1 - x_hi)
-        return remote(turned.at[j, ct], halves.at[x_lo, zs % 2, core], x_send.at[j, ct],
-                      x_recv.at[x_lo, zs % 2, core], dp_of(tok_hi, z, ct), x_hi * 4 + zs // 2)
+    def x_copy(zp, ct):
+        tok_hi = jnp.where(core == 0, x_hi, 1 - x_hi)
+        return remote(turned.at[zp, ct], halves.at[x_lo, zp], x_send.at[zp, ct],
+                      x_recv.at[x_lo, zp], dp_of(tok_hi, z, ct), x_hi * 4 + y)
+
+    def near_self(ct):
+        return jnp.logical_and(x_lo == x_hi, jnp.logical_and(core == 0, ct == 0))
 
     def to_self(j, g, ct):
         same = jnp.logical_and(g == 0, x_lo == x_hi)
@@ -336,37 +373,87 @@
     def active(j, g):
         return summer(j, g) == y
 
-    def stage_two(j, g):
-        for k in range(1, 4):
-            ys = (y + k) % 4
-            for part in range(2):
-                lanes = pl.ds(*PARTS[part])
-                remote(outgoing.at[0, 0, :, lanes], arrived.at[j, ys, :, lanes], y_send.at[0, 0, part],
-                       y_recv.at[j, ys, part], dp, tensor).wait_recv()
-        total = arrived[j, 0].astype(F32)
-        for ys in range(1, 4):
-            total = total + arrived[j, ys].astype(F32)
-        total = total.astype(BF)
+    def stage_near(zp):
+        parts = [[], []]
+        for cs in range(2):
+            for k in range(4):
+                ys = (y + k) % 4
+
+                def arrive(ys=ys, cs=cs):
+                    for part in range(2):
+                        lanes = pl.ds(*PARTS[part])
+                        remote(outgoing.at[0, 0, :, lanes], arrived.at[zp, ys, cs, :, lanes], y_send.at[0, 0, part],
+                               y_recv.at[zp, ys, cs, part], dp, tensor).wait_recv()
+                if k == 0:
+                    pl.when(core != cs)(arrive)
+                else:
+                    arrive()
+            total = arrived[zp, 0, cs].astype(F32)
+            for ys in range(1, 4):
+                total = total + arrived[zp, ys, cs].astype(F32)
+            total = total.astype(BF)
+            for ct in range(2):
+                parts[ct] += [total[:, ct * FIRST:(ct + 1) * FIRST],
+                              total[:, 2 * FIRST + ct * LAST:2 * FIRST + (ct + 1) * LAST]]
         for ct in range(2):
-            part = jnp.concatenate(
-                [total[:, ct * FIRST:(ct + 1) * FIRST],
-                 total[:, 2 * FIRST + ct * LAST:2 * FIRST + (ct + 1) * LAST]], axis=1)
-            mine_too = to_self(j, g, ct)
-
-            @pl.when(mine_too)
+            both = jnp.concatenate(parts[ct], axis=1)
+
+            @pl.when(near_self(ct))
             def _():
-                halves[x_lo, zsrc_of(j) % 2, core] = part
-
-            @pl.when(jnp.logical_not(mine_too))
+                halves[x_lo, zp] = both
+
+            @pl.when(jnp.logical_not(near_self(ct)))
             def _():
-                turned[j, ct] = part
-                x_copy(j, g, ct).start()
+                turned[zp, ct] = both
+                x_copy(zp, ct).start()
+
+    def f_copy(j, g, ct, part):
+        zs = zsrc_of(j)
+        tok_hi = jnp.where(g == 0, x_hi, 1 - x_hi)
+        src, dst = ((turned_a, whole_a), (turned_b, whole_b))[part]
+        return remote(src.at[j - WHOLE, ct], dst.at[zs % 2, core], f_send.at[j, ct],
+                      f_recv.at[zs % 2, core, part], dp_of(tok_hi, z, ct), x_hi * 4 + zs // 2)
+
+    def stage_whole(j, g):
+        for part in range(2):
+            @pl.when(share_lo(g, part) == x_lo)
+            def _(part=part):
+                n = PARTS[part][1]
+                for k in range(1, 8):
+                    frm = (tensor + k) % 8
+                    remote(outgoing.at[0, 0, :, pl.ds(0, n)], arrived_w.at[j - WHOLE, frm, :, pl.ds(0, n)],
+                           y_send.at[0, 0, part], e_recv.at[j, frm], dp, tensor).wait_recv()
+                total = arrived_w[j - WHOLE, 0, :, 0:n].astype(F32)
+                for k in range(1, 8):
+                    total = total + arrived_w[j - WHOLE, k, :, 0:n].astype(F32)
+                total = total.astype(BF)
+                src, dst = ((turned_a, whole_a), (turned_b, whole_b))[part]
+                for ct in range(2):
+                    piece = total[:, ct * (n // 2):(ct + 1) * (n // 2)]
+                    mine_too = to_self(j, g, ct)
+
+                    @pl.when(mine_too)
+                    def _():
+                        dst[zsrc_of(j) % 2, core] = piece
+
+                    @pl.when(jnp.logical_not(mine_too))
+                    def _():
+                        src[j - WHOLE, ct] = piece
+                        f_copy(j, g, ct, part).start()
 
     def second(lo, hi, g):
         def unit(j, carry):
-            pl.when(active(j, g))(lambda: stage_two(j, g))
+            pl.when(active(j, g))(lambda: stage_whole(j, g))
             return carry
         lax.fori_loop(lo, hi, unit, 0)
+
+    def near_units(which, lo, hi):
+        def unit(zp, carry):
+            step = steps_of(zp)
+            here = jnp.logical_and(jnp.logical_and(step >= lo, step <= hi), core == which)
+            pl.when(here)(lambda: stage_near(zp))
+            return carry
+        lax.fori_loop(0, 2, unit, 0)
 
     def steps_of(zp):
         away = (2 * y + zp - z + 8) % 8
@@ -377,10 +464,20 @@
             place[part].wait()
             to_other[part].wait_recv()
     items(0, 1, 0)
+    pl.semaphore_wait(met.at[1], 2)
+    tell(4)
+
+    def publish_when_met():
+        pl.semaphore_wait(met.at[2], 1)
+        publish()
     with jax.named_scope("a1_publish"):
-        pl.when(owner == tensor)(publish)
+        pl.when(owner == tensor)(publish_when_met)
     with jax.named_scope("a2_ring10"):
         ring(1, 0)
+
+    @pl.when(owner != tensor)
+    def _():
+        pl.semaphore_wait(met.at[2], 1)
     with jax.named_scope("a3_ring11"):
         ring(1, 1)
     items(1, 3, 0)
@@ -392,9 +489,6 @@
     with jax.named_scope("a6_relay0"):
         relay[0].wait_recv()
     items(0, 3, 1, (0,))
-    with jax.named_scope("a7_receive"):
-        receive()
-    backward()
     with jax.named_scope("a8_ring21"):
         ring(2, 1)
     items(3, 5, 0)
@@ -402,52 +496,73 @@
     with jax.named_scope("a9_far1"):
         to_far[1].wait_recv()
     relay[1].start()
-    second(0, 3, 0)
+    with jax.named_scope("aa_receive"):
+        receive()
+    backward()
     with jax.named_scope("aa_relay1"):
         relay[1].wait_recv()
     items(0, 5, 1, (1,))
     with jax.named_scope("ab_ring30"):
         ring(3, 0)
-    with jax.named_scope("b0_grads"):
-        gradients()
+    with jax.named_scope("ac_near"):
+        near_units(0, 0, 1)
     with jax.named_scope("b1_ring31"):
         ring(3, 1)
     with jax.named_scope("b2_items"):
         items_both(5, 7)
-    with jax.named_scope("b3_plane"):
-        sum_plane()
-    with jax.named_scope("b4_second"):
-        second(3, 5, 0)
+    with jax.named_scope("b3_grads"):
+        gradients()
     with jax.named_scope("b5_last"):
         w_copy(0, 4, 0).wait_recv()
         w_copy(1, 4, 1).wait_recv()
     with jax.named_scope("b6_items"):
         items_both(7, 8)
-    with jax.named_scope("b8_second"):
-        second(0, 5, 1)
-    with jax.named_scope("b9_second"):
+    with jax.named_scope("b7_second"):
         second(5, 7, 0)
         second(5, 7, 1)
+    with jax.named_scope("b8_near"):
+        near_units(0, 2, 2)
+        near_units(1, 0, 1)
     with jax.named_scope("ba_second"):
         second(7, 8, 0)
         second(7, 8, 1)
+    with jax.named_scope("bb_near"):
+        near_units(1, 2, 2)
 
     def finish(i, carry):
         zp = jnp.where(steps_of(0) <= steps_of(1), i, 1 - i)
-        parts = []
-        for cs in range(2):
+        away = jnp.where(x_lo == x_hi, 0, 1)
+        whole = steps_of(zp) >= FAR
+
+        @pl.when(jnp.logical_not(whole))
+        def _():
             for xl in range(2):
-                far = jnp.where(x_lo == x_hi, 0, 1)
-                frm = (2 * y + zp + 2 * far + cs) % 4
-                own = jnp.logical_and(jnp.logical_and(x_lo == x_hi, xl == x_lo),
-                                      jnp.logical_and(frm == y, core == cs))
-
-                @pl.when(jnp.logical_not(own))
+                own_part = jnp.logical_and(jnp.logical_and(x_lo == x_hi, xl == x_lo), core == 0)
+
+                @pl.when(jnp.logical_not(own_part))
                 def _():
-                    remote(turned.at[0, 0], halves.at[xl, zp, cs], x_send.at[0, 0], x_recv.at[xl, zp, cs],
+                    remote(turned.at[0, 0], halves.at[xl, zp], x_send.at[0, 0], x_recv.at[xl, zp],
                            dp, tensor).wait_recv()
-            parts.append(halves[0, zp, cs].astype(F32) + halves[1, zp, cs].astype(F32))
-        pre = extra[zp] + jnp.concatenate(parts, axis=0).T
+            both = halves[0, zp].astype(F32) + halves[1, zp].astype(F32)
+            for cs in range(2):
+                flat[cs * COLS:(cs + 1) * COLS, :] = both[:, cs * TOK:(cs + 1) * TOK]
+
+        @pl.when(whole)
+        def _():
+            for cs in range(2):
+                for part in range(2):
+                    frm = (2 * y + zp + 2 * away + cs) % 4
+                    own_part = jnp.logical_and(jnp.logical_and(x_lo == x_hi, (part + away) % 2 == x_lo),
+                                               jnp.logical_and(frm == y, core == cs))
+                    src, dst = ((turned_a, whole_a), (turned_b, whole_b))[part]
+
+                    @pl.when(jnp.logical_not(own_part))
+                    def _():
+                        remote(src.at[0, 0], dst.at[zp, cs], f_send.at[0, 0], f_recv.at[zp, cs, part],
+                               dp, tensor).wait_recv()
+                flat[cs * COLS:(cs + 1) * COLS, 0:FIRST] = whole_a[zp, cs].astype(F32)
+                flat[cs * COLS:(cs + 1) * COLS, FIRST:TOK] = whole_b[zp, cs].astype(F32)
+        pre = extra[zp] + flat[...].T
         sums[zp] = jnp.sum(cots[zp] * pre, axis=0, keepdims=True) / norms[zp]
         results[zp] = pre * scales[zp]
         return carry
@@ -465,11 +580,13 @@
         return carry
     with jax.named_scope("c1_mag"):
         lax.fori_loop(1, 32, mag_start, 0)
-    with jax.named_scope("b7_planes"):
-        sum_planes()
+    with jax.named_scope("c3_plane"):
+        sum_plane()
     with jax.named_scope("c2_mixed"):
         for zp in range(2):
             mixed_ref[:, HALF * zp:HALF * (zp + 1)] = results[zp].astype(BF)
+    with jax.named_scope("c4_planes"):
+        sum_planes()
 
     for k in (1, 2, 3, 4):
         for side in (0, 1):
@@ -500,27 +617,39 @@
             copies[part].wait_send()
     def drain(j, carry):
         for g in range(2):
-            @pl.when(jnp.logical_not(local(j, g)))
+            @pl.when(jnp.logical_not(local_near(j, g)))
             def _():
                 for part in range(2):
                     y_copy(j, g, part).wait_send()
         return carry
-    lax.fori_loop(0, 8, drain, 0)
-
-    def drain_two(j, carry):
+    lax.fori_loop(0, WHOLE, drain, 0)
+
+    def drain_near(zp, carry):
+        for ct in range(2):
+            @pl.when(jnp.logical_and(steps_of(zp) < FAR, jnp.logical_not(near_self(ct))))
+            def _():
+                x_copy(zp, ct).wait_send()
+        return carry
+    lax.fori_loop(0, 2, drain_near, 0)
+
+    def drain_whole(j, carry):
         for g in range(2):
-            for ct in range(2):
-                @pl.when(jnp.logical_and(active(j, g), jnp.logical_not(to_self(j, g, ct))))
+            for part in range(2):
+                @pl.when(jnp.logical_not(local_whole(j, g, part)))
                 def _():
-                    x_copy(j, g, ct).wait_send()
+                    e_copy(j, g, part).wait_send()
+                for ct in range(2):
+                    @pl.when(jnp.logical_and(local_whole(j, g, part), jnp.logical_not(to_self(j, g, ct))))
+                    def _():
+                        f_copy(j, g, ct, part).wait_send()
         return carry
-    lax.fori_loop(0, 8, drain_two, 0)
+    lax.fori_loop(WHOLE, 8, drain_whole, 0)
 
     def mag_arrive(i, total):
         frm = (dp + i) % 32
         remote(mag_out.at[0], mag_in.at[frm], g_send.at[0], g_recv.at[frm], dp, tensor).wait_recv()
         return total + mag_in[frm]
-    with jax.named_scope("c3_gmag"):
+    with jax.named_scope("c5_gmag"):
         gmag_ref[...] = lax.fori_loop(1, 32, mag_arrive, mag_out[dp])
 
     def mag_sent(i, carry):
@@ -530,23 +659,23 @@
 
 
 def body(hidden, weight, factor_b, factor_a, magnitude, cotangent):
-    any_spec, vmem_spec = pl.BlockSpec(memory_space=pl.ANY), pl.BlockSpec(memory_space=pltpu.VMEM)
+    hbm_spec, vmem_spec = pl.BlockSpec(memory_space=pltpu.HBM), pl.BlockSpec(memory_space=pltpu.VMEM)
     dma, vmem = pltpu.SemaphoreType.DMA, pltpu.VMEM
     mixed, grads, gmag = pl.pallas_call(
         kernel,
         name="dora",
         out_shape=(jax.ShapeDtypeStruct((TOK, OUT), BF), jax.ShapeDtypeStruct((16, 128), F32),
                    jax.ShapeDtypeStruct((1, 128), F32)),
-        in_specs=[any_spec] * 6,
+        in_specs=[hbm_spec] * 6,
         out_specs=(vmem_spec,) * 3,
         scratch_shapes=[
             vmem((16, HID), BF), vmem((16, COLS), BF), vmem((OUT,), F32), vmem((TOK, OUT), BF), vmem((TOK, HID), BF),
             vmem((2, 2 * TOK, HID), BF),
             vmem((8, COLS, HID), BF),
             vmem((8, 2, COLS, 2 * TOK), BF),
-            vmem((8, 4, COLS, 2 * TOK), BF),
-            vmem((8, 2, COLS, TOK), BF),
-            vmem((2, 2, 2, COLS, TOK), BF),
+            vmem((2, 4, 2, COLS, 2 * TOK), BF),
+            vmem((2, 2, COLS, 2 * TOK), BF),
+            vmem((2, 2, COLS, 2 * TOK), BF),
             vmem((8, COLS), F32), vmem((8, 8, COLS), F32),
             vmem((16, 256), F32), vmem((16, 256), BF), vmem((4, 16, 256), BF),
             vmem((2, 16, HALF), F32), vmem((2, 1, HALF), F32), vmem((2, 1, HALF), F32), vmem((2, 1, HALF), F32),
@@ -556,9 +685,13 @@
             vmem((8, 16, 128), F32), vmem((8, 16, 128), F32),
             vmem((32, 1, 128), F32), vmem((32, 1, 128), F32), vmem((2, 1, HALF), F32), vmem((2, TOK, HALF), F32),
             dma((8,)), dma((2, 4, 2)), dma((8, 2)), dma((3, 2)), dma((3, 2)),
-            dma((8, 2, 2)), dma((8, 4, 2)), dma((8, 2)), dma((2, 2, 2)),
+            dma((8, 2, 2)), dma((2, 4, 2, 2)), dma((2, 2)), dma((2, 2)),
             dma((1,)), dma((8,)), dma((32,)), dma((4,)), dma((8,)), dma((8,)), dma((8,)), dma((8,)),
             dma((4,)), dma((4,)), dma((8,)), dma((8,)), dma((32,)), dma((32,)),
+            vmem((8 - WHOLE, 8, COLS, 2 * FIRST), BF),
+            vmem((8 - WHOLE, 2, COLS, FIRST), BF), vmem((8 - WHOLE, 2, COLS, LAST), BF),
+            vmem((2, 2, COLS, FIRST), BF), vmem((2, 2, COLS, LAST), BF), vmem((2 * COLS, TOK), F32),
+            dma((8, 8)), dma((8, 2)), dma((2, 2, 2)), pltpu.SemaphoreType.REGULAR((3,)),
         ],
         compiler_params=pltpu.CompilerParams(
             collective_id=0, has_side_effects=True, vmem_limit_bytes=48 * 1024 * 1024

time: 114 us -> 118 us (1.035)
  the two profiles are of different devices: /device:TPU:1 before, /device:TPU:25 now
where the time goes in v4:
time: 118 us
  Pallas kernels  109 us (92%)
  local copies, waits for them, and re-layouts  8.26 us (7%)
    pallas_call x1, Pallas kernels, body(): pl.pallas_call(kernel, name='dora', out_shape=(jax.ShapeDtypeStruct((TOK,...  109 us
    unnamed x13, local copies, waits for them, and re-layouts  6.47 us

profile of v4, /device:TPU:25, one launch (start us, length us, event | category | flops | bytes accessed | tf_op | source)
XLA Modules:
  0.0 118.0 jit_solution(8254828384075515342)
XLA Ops:
  0.6 0.0 copy-start
  0.6 1.4 %copy-done = bf16[320,2304]{1,0:T(8,128)(2,1)S(1)} copy-done((bf16[320,2304]{1,0:T(8,128)(2,1)S(1)}, bf16[320,2304]{1,0:T(8,128)(2,1)}, u32[]{:S(2)}) %copy-start) | copy-done | bytes 1474584
  2.0 0.0 copy-start.1
  2.0 1.1 copy-done.1
  3.1 0.0 copy-start.2
  3.1 1.0 copy-done.2
  4.1 0.0 copy-start.3
  4.1 0.9 copy-done.3
  5.0 0.0 copy-start.4
  5.0 0.7 copy-done.4
  5.7 0.0 copy-start.5
  5.7 0.7 copy-done.5
  6.4 109.1 %dora.1 = (bf16[320,576]{1,0:T(8,128)(2,1)S(1)}, f32[16,128]{1,0:T(8,128)S(1)}, f32[1,128]{1,0:T(1,128)S(1)}) custom-call(bf16[320,2304]{1,0:T(8,128)(2,1)S(1)} %copy-done, bf16[144,2304]{1,0:T(8,128)(2,1)S(1)} %bitcast.6, bf16[16,2304]{1,0:T(8,128)(2,1)S(1)} %bitcast.7, bf16[16,144]{1,0:T(8,128)(2,1)S(1)} %copy-done.4, f32[576]{0:T(1024)S(1)} %copy-done.5, ...), custom_call_target="tpu_custom_call" | custom-call | tf_op jit(solution)/shard_map/dora/pallas_call | solution.py:664
  115.4 0.5 slice_bitcast_fusion.1
  116.0 0.6 slice_bitcast_fusion
  116.6 0.7 slice.10
  117.2 0.8 copy.11
Async XLA Ops:
  0.6 1.4 %copy-start = (bf16[320,2304]{1,0:T(8,128)(2,1)S(1)}, bf16[320,2304]{1,0:T(8,128)(2,1)}, u32[]{:S(2)}) copy-start(bf16[320,2304]{1,0:T(8,128)(2,1)} %h_ref.1) | copy-start | bytes 4423684
  2.0 1.1 copy-start.1
  3.1 1.0 copy-start.2
  4.1 0.9 copy-start.3
  5.0 0.7 copy-start.4
  5.7 0.7 copy-start.5

commit v5 on v4

--- a/solution.py
+++ b/solution.py
@@ -13,8 +13,8 @@
 CHUNKS = ((0, 80), (80, 64))
 FIRST, LAST = 192, 128
 PARTS = ((0, 2 * FIRST), (2 * FIRST, 2 * LAST))
-WHOLE = 5
-FAR = (WHOLE + 1) // 2
+WHOLE = 8
+FAR = WHOLE // 2 + 1
 
 
 def remote(src, dst, send, recv, dp, tensor):
@@ -165,16 +165,16 @@
         k = (j + 1) // 2
         return (z + 8 + k - 2 * k * (j % 2)) % 8
 
+    def summer_at(owner_y, g, of):
+        return (owner_y + jnp.where(g == 0, 3 - 2 * of, 2 * of)) % 4
+
     def summer(j, g):
-        return (zsrc_of(j) + 2 * g + core) % 4
+        return summer_at(zsrc_of(j) // 2, g, core)
 
     def y_copy(j, g, part):
-        zs, lanes = zsrc_of(j), pl.ds(*PARTS[part])
-        return remote(outgoing.at[j, g, :, lanes], arrived.at[zs % 2, y, core, :, lanes], y_send.at[j, g, part],
-                      y_recv.at[zs % 2, y, core, part], dp_of(x_hi, z, g), x_lo * 4 + zs // 2)
-
-    def local_near(j, g):
-        return jnp.logical_and(zsrc_of(j) // 2 == y, core == g)
+        lanes = pl.ds(*PARTS[part])
+        return remote(outgoing.at[j, g, :, lanes], arrived.at[j, y, :, lanes], y_send.at[j, g, part],
+                      y_recv.at[j, y, part], dp, x_lo * 4 + summer(j, g))
 
     def local(j, g):
         return summer(j, g) == y
@@ -209,11 +209,11 @@
                     outgoing[j, g, :, at:at + n] = piece
                     e_copy(j, g, part).start()
             return
-        here = local_near(j, g)
+        here = local(j, g)
 
         @pl.when(here)
         def _():
-            arrived[zsrc_of(j) % 2, y, core, :, lo:hi] = p
+            arrived[j, y, :, lo:hi] = p
 
         @pl.when(jnp.logical_not(here))
         def _():
@@ -358,13 +358,11 @@
             if k < 3 or first == 0:
                 w_copy(side, k + 1, ch).start()
 
-    def x_copy(zp, ct):
-        tok_hi = jnp.where(core == 0, x_hi, 1 - x_hi)
-        return remote(turned.at[zp, ct], halves.at[x_lo, zp], x_send.at[zp, ct],
-                      x_recv.at[x_lo, zp], dp_of(tok_hi, z, ct), x_hi * 4 + y)
-
-    def near_self(ct):
-        return jnp.logical_and(x_lo == x_hi, jnp.logical_and(core == 0, ct == 0))
+    def x_copy(j, g, ct):
+        zs = zsrc_of(j)
+        tok_hi = jnp.where(g == 0, x_hi, 1 - x_hi)
+        return remote(turned.at[j, ct], halves.at[x_lo, zs % 2, core], x_send.at[j, ct],
+                      x_recv.at[x_lo, zs % 2, core], dp_of(tok_hi, z, ct), x_hi * 4 + zs // 2)
 
     def to_self(j, g, ct):
         same = jnp.logical_and(g == 0, x_lo == x_hi)
@@ -373,39 +371,31 @@
     def active(j, g):
         return summer(j, g) == y
 
-    def stage_near(zp):
-        parts = [[], []]
-        for cs in range(2):
-            for k in range(4):
-                ys = (y + k) % 4
-
-                def arrive(ys=ys, cs=cs):
-                    for part in range(2):
-                        lanes = pl.ds(*PARTS[part])
-                        remote(outgoing.at[0, 0, :, lanes], arrived.at[zp, ys, cs, :, lanes], y_send.at[0, 0, part],
-                               y_recv.at[zp, ys, cs, part], dp, tensor).wait_recv()
-                if k == 0:
-                    pl.when(core != cs)(arrive)
-                else:
-                    arrive()
-            total = arrived[zp, 0, cs].astype(F32)
-            for ys in range(1, 4):
-                total = total + arrived[zp, ys, cs].astype(F32)
-            total = total.astype(BF)
-            for ct in range(2):
-                parts[ct] += [total[:, ct * FIRST:(ct + 1) * FIRST],
-                              total[:, 2 * FIRST + ct * LAST:2 * FIRST + (ct + 1) * LAST]]
+    def stage_two(j, g):
+        for k in range(1, 4):
+            ys = (y + k) % 4
+            for part in range(2):
+                lanes = pl.ds(*PARTS[part])
+                remote(outgoing.at[0, 0, :, lanes], arrived.at[j, ys, :, lanes], y_send.at[0, 0, part],
+                       y_recv.at[j, ys, part], dp, tensor).wait_recv()
+        total = arrived[j, 0].astype(F32)
+        for ys in range(1, 4):
+            total = total + arrived[j, ys].astype(F32)
+        total = total.astype(BF)
         for ct in range(2):
-            both = jnp.concatenate(parts[ct], axis=1)
-
-            @pl.when(near_self(ct))
+            part = jnp.concatenate(
+                [total[:, ct * FIRST:(ct + 1) * FIRST],
+                 total[:, 2 * FIRST + ct * LAST:2 * FIRST + (ct + 1) * LAST]], axis=1)
+            mine_too = to_self(j, g, ct)
+
+            @pl.when(mine_too)
             def _():
-                halves[x_lo, zp] = both
-
-            @pl.when(jnp.logical_not(near_self(ct)))
+                halves[x_lo, zsrc_of(j) % 2, core] = part
+
+            @pl.when(jnp.logical_not(mine_too))
             def _():
-                turned[zp, ct] = both
-                x_copy(zp, ct).start()
+                turned[j, ct] = part
+                x_copy(j, g, ct).start()
 
     def f_copy(j, g, ct, part):
         zs = zsrc_of(j)
@@ -442,18 +432,13 @@
                         f_copy(j, g, ct, part).start()
 
     def second(lo, hi, g):
-        def unit(j, carry):
-            pl.when(active(j, g))(lambda: stage_whole(j, g))
-            return carry
-        lax.fori_loop(lo, hi, unit, 0)
-
-    def near_units(which, lo, hi):
-        def unit(zp, carry):
-            step = steps_of(zp)
-            here = jnp.logical_and(jnp.logical_and(step >= lo, step <= hi), core == which)
-            pl.when(here)(lambda: stage_near(zp))
-            return carry
-        lax.fori_loop(0, 2, unit, 0)
+        for a, b, whole in split(lo, hi):
+            stage = stage_whole if whole else stage_two
+
+            def unit(j, carry, stage=stage):
+                pl.when(active(j, g))(lambda: stage(j, g))
+                return carry
+            lax.fori_loop(a, b, unit, 0)
 
     def steps_of(zp):
         away = (2 * y + zp - z + 8) % 8
@@ -499,35 +484,34 @@
     with jax.named_scope("aa_receive"):
         receive()
     backward()
-    with jax.named_scope("aa_relay1"):
+    with jax.named_scope("aa_second"):
+        second(0, 3, 0)
+    with jax.named_scope("ab_relay1"):
         relay[1].wait_recv()
     items(0, 5, 1, (1,))
-    with jax.named_scope("ab_ring30"):
+    with jax.named_scope("ac_ring30"):
         ring(3, 0)
-    with jax.named_scope("ac_near"):
-        near_units(0, 0, 1)
     with jax.named_scope("b1_ring31"):
         ring(3, 1)
     with jax.named_scope("b2_items"):
         items_both(5, 7)
-    with jax.named_scope("b3_grads"):
-        gradients()
     with jax.named_scope("b5_last"):
         w_copy(0, 4, 0).wait_recv()
         w_copy(1, 4, 1).wait_recv()
     with jax.named_scope("b6_items"):
         items_both(7, 8)
     with jax.named_scope("b7_second"):
+        second(3, 5, 0)
+    with jax.named_scope("b8_grads"):
+        gradients()
+    with jax.named_scope("b9_second"):
+        second(0, 5, 1)
+    with jax.named_scope("ba_second"):
         second(5, 7, 0)
         second(5, 7, 1)
-    with jax.named_scope("b8_near"):
-        near_units(0, 2, 2)
-        near_units(1, 0, 1)
-    with jax.named_scope("ba_second"):
+    with jax.named_scope("bb_second"):
         second(7, 8, 0)
         second(7, 8, 1)
-    with jax.named_scope("bb_near"):
-        near_units(1, 2, 2)
 
     def finish(i, carry):
         zp = jnp.where(steps_of(0) <= steps_of(1), i, 1 - i)
@@ -536,22 +520,23 @@
 
         @pl.when(jnp.logical_not(whole))
         def _():
-            for xl in range(2):
-                own_part = jnp.logical_and(jnp.logical_and(x_lo == x_hi, xl == x_lo), core == 0)
-
-                @pl.when(jnp.logical_not(own_part))
-                def _():
-                    remote(turned.at[0, 0], halves.at[xl, zp], x_send.at[0, 0], x_recv.at[xl, zp],
-                           dp, tensor).wait_recv()
-            both = halves[0, zp].astype(F32) + halves[1, zp].astype(F32)
             for cs in range(2):
-                flat[cs * COLS:(cs + 1) * COLS, :] = both[:, cs * TOK:(cs + 1) * TOK]
+                for xl in range(2):
+                    frm = summer_at(y, away, cs)
+                    own_part = jnp.logical_and(jnp.logical_and(x_lo == x_hi, xl == x_lo),
+                                               jnp.logical_and(frm == y, core == cs))
+
+                    @pl.when(jnp.logical_not(own_part))
+                    def _():
+                        remote(turned.at[0, 0], halves.at[xl, zp, cs], x_send.at[0, 0], x_recv.at[xl, zp, cs],
+                               dp, tensor).wait_recv()
+                flat[cs * COLS:(cs + 1) * COLS, :] = halves[0, zp, cs].astype(F32) + halves[1, zp, cs].astype(F32)
 
         @pl.when(whole)
         def _():
             for cs in range(2):
                 for part in range(2):
-                    frm = (2 * y + zp + 2 * away + cs) % 4
+                    frm = summer_at(y, away, cs)
                     own_part = jnp.logical_and(jnp.logical_and(x_lo == x_hi, (part + away) % 2 == x_lo),
                                                jnp.logical_and(frm == y, core == cs))
                     src, dst = ((turned_a, whole_a), (turned_b, whole_b))[part]
@@ -580,7 +565,7 @@
         return carry
     with jax.named_scope("c1_mag"):
         lax.fori_loop(1, 32, mag_start, 0)
-    with jax.named_scope("c3_plane"):
+    with jax.named_scope("c2_plane"):
         sum_plane()
     with jax.named_scope("c2_mixed"):
         for zp in range(2):
@@ -617,20 +602,16 @@
             copies[part].wait_send()
     def drain(j, carry):
         for g in range(2):
-            @pl.when(jnp.logical_not(local_near(j, g)))
+            @pl.when(jnp.logical_not(local(j, g)))
             def _():
                 for part in range(2):
                     y_copy(j, g, part).wait_send()
+            for ct in range(2):
+                @pl.when(jnp.logical_and(active(j, g), jnp.logical_not(to_self(j, g, ct))))
+                def _():
+                    x_copy(j, g, ct).wait_send()
         return carry
     lax.fori_loop(0, WHOLE, drain, 0)
-
-    def drain_near(zp, carry):
-        for ct in range(2):
-            @pl.when(jnp.logical_and(steps_of(zp) < FAR, jnp.logical_not(near_self(ct))))
-            def _():
-                x_copy(zp, ct).wait_send()
-        return carry
-    lax.fori_loop(0, 2, drain_near, 0)
 
     def drain_whole(j, carry):
         for g in range(2):
@@ -673,9 +654,9 @@
             vmem((2, 2 * TOK, HID), BF),
             vmem((8, COLS, HID), BF),
             vmem((8, 2, COLS, 2 * TOK), BF),
-            vmem((2, 4, 2, COLS, 2 * TOK), BF),
-            vmem((2, 2, COLS, 2 * TOK), BF),
-            vmem((2, 2, COLS, 2 * TOK), BF),
+            vmem((WHOLE, 4, COLS, 2 * TOK), BF),
+            vmem((WHOLE, 2, COLS, TOK), BF),
+            vmem((2, 2, 2, COLS, TOK), BF),
             vmem((8, COLS), F32), vmem((8, 8, COLS), F32),
             vmem((16, 256), F32), vmem((16, 256), BF), vmem((4, 16, 256), BF),
             vmem((2, 16, HALF), F32), vmem((2, 1, HALF), F32), vmem((2, 1, HALF), F32), vmem((2, 1, HALF), F32),
@@ -685,16 +666,16 @@
             vmem((8, 16, 128), F32), vmem((8, 16, 128), F32),
             vmem((32, 1, 128), F32), vmem((32, 1, 128), F32), vmem((2, 1, HALF), F32), vmem((2, TOK, HALF), F32),
             dma((8,)), dma((2, 4, 2)), dma((8, 2)), dma((3, 2)), dma((3, 2)),
-            dma((8, 2, 2)), dma((2, 4, 2, 2)), dma((2, 2)), dma((2, 2)),
+            dma((8, 2, 2)), dma((8, 4, 2)), dma((8, 2)), dma((2, 2, 2)),
             dma((1,)), dma((8,)), dma((32,)), dma((4,)), dma((8,)), dma((8,)), dma((8,)), dma((8,)),
             dma((4,)), dma((4,)), dma((8,)), dma((8,)), dma((32,)), dma((32,)),
-            vmem((8 - WHOLE, 8, COLS, 2 * FIRST), BF),
-            vmem((8 - WHOLE, 2, COLS, FIRST), BF), vmem((8 - WHOLE, 2, COLS, LAST), BF),
+            vmem((max(8 - WHOLE, 1), 8, COLS, 2 * FIRST), BF),
+            vmem((max(8 - WHOLE, 1), 2, COLS, FIRST), BF), vmem((max(8 - WHOLE, 1), 2, COLS, LAST), BF),
             vmem((2, 2, COLS, FIRST), BF), vmem((2, 2, COLS, LAST), BF), vmem((2 * COLS, TOK), F32),
             dma((8, 8)), dma((8, 2)), dma((2, 2, 2)), pltpu.SemaphoreType.REGULAR((3,)),
         ],
         compiler_params=pltpu.CompilerParams(
-            collective_id=0, has_side_effects=True, vmem_limit_bytes=48 * 1024 * 1024
+            collective_id=0, has_side_effects=True, vmem_limit_bytes=67043328
         ),
     )(hidden, weight.T, factor_b.T, factor_a, magnitude, cotangent)
     return mixed, gmag[0, :18], grads[:, 72:90], grads[:, :72].T

time: 118 us -> 109 us (0.924)
  the two profiles are of different devices: /device:TPU:25 before, /device:TPU:1 now
where the time goes in v5:
time: 109 us; the launch traced here: 108 us
  Pallas kernels  102 us (94%)
  local copies, waits for them, and re-layouts  5.57 us (5%)
    pallas_call x1, Pallas kernels, body(): pl.pallas_call(kernel, name='dora', out_shape=(jax.ShapeDtypeStruct((TOK,...  102 us

profile of v5, /device:TPU:1, one launch (start us, length us, event | category | flops | bytes accessed | tf_op | source)
XLA Modules:
  0.0 108.4 jit_solution(10388364389970923321)
XLA Ops:
  0.6 102.2 %dora.1 = (bf16[320,576]{1,0:T(8,128)(2,1)}, f32[16,128]{1,0:T(8,128)}, f32[1,128]{1,0:T(1,128)}) custom-call(bf16[320,2304]{1,0:T(8,128)(2,1)} %h_ref.1, bf16[144,2304]{1,0:T(8,128)(2,1)} %bitcast.6, bf16[16,2304]{1,0:T(8,128)(2,1)} %bitcast.7, bf16[16,144]{1,0:T(8,128)(2,1)} %a_hbm.1, f32[576]{0:T(1024)} %mag_hbm.1, bf16[320,576]{1,0:T(8,128)(2,1)} %cot_hbm.1), custom_call_target="tpu_custom_call" | custom-call | tf_op jit(solution)/shard_map/dora/pallas_call | solution.py:645
  102.8 1.1 %slice_bitcast_fusion.1 = f32[18]{0:T(128)} fusion(f32[1,128]{1,0:T(1,128)} %get-tuple-element.8), kind=kLoop, calls=%fused_computation.1 | loop fusion | bytes 144 | tf_op jit(solution)/shard_map/squeeze | solution.py:681
  103.9 1.3 %slice_bitcast_fusion = f32[72,16]{0,1:T(8,128)} fusion(f32[16,128]{1,0:T(8,128)} %get-tuple-element.9), kind=kLoop, calls=%fused_computation | loop fusion | bytes 9216 | tf_op jit(solution)/shard_map/transpose | solution.py:681
  105.2 1.4 %slice.10 = f32[16,18]{1,0:T(8,128)} slice(f32[16,128]{1,0:T(8,128)} %get-tuple-element.9), slice={[0:16], [72:90]} | slice | bytes 2304 | tf_op jit(solution)/shard_map/slice | solution.py:681
  106.6 1.8 %copy.11 = bf16[320,576]{1,0:T(8,128)(2,1)} copy(bf16[320,576]{1,0:T(8,128)(2,1)} %get-tuple-element.14) | data formatting | bytes 737280

commit v6 on v5

--- a/solution.py
+++ b/solution.py
@@ -13,8 +13,6 @@
 CHUNKS = ((0, 80), (80, 64))
 FIRST, LAST = 192, 128
 PARTS = ((0, 2 * FIRST), (2 * FIRST, 2 * LAST))
-WHOLE = 8
-FAR = WHOLE // 2 + 1
 
 
 def remote(src, dst, send, recv, dp, tensor):
@@ -32,7 +30,7 @@
            loc_sem, w_send, w_recv, t_send, t_recv, y_send, y_recv, x_send, x_recv,
            s_send, s_recv, m_send, m_recv, l_send, l_recv, b_send, b_recv, d_send, d_recv, p_send, p_recv,
            g_send, g_recv,
-           arrived_w, turned_a, turned_b, whole_a, whole_b, flat, e_recv, f_send, f_recv, met):
+           met):
     dp, tensor = lax.axis_index("dp"), lax.axis_index("tensor")
     x_hi, z, core = dp // 16, (dp // 2) % 8, dp % 2
     x_lo, y = tensor // 4, tensor % 4
@@ -179,36 +177,10 @@
     def local(j, g):
         return summer(j, g) == y
 
-    def share_lo(g, part):
-        return (part + g) % 2
-
-    def e_copy(j, g, part):
-        at, n = PARTS[part]
-        return remote(outgoing.at[j, g, :, pl.ds(at, n)], arrived_w.at[j - WHOLE, tensor, :, pl.ds(0, n)],
-                      y_send.at[j, g, part], e_recv.at[j, tensor], dp, share_lo(g, part) * 4 + summer(j, g))
-
-    def local_whole(j, g, part):
-        return jnp.logical_and(local(j, g), share_lo(g, part) == x_lo)
-
-    def item(j, g, parts, whole):
+    def item(j, g, parts):
         lo, hi = PARTS[parts[0]][0], sum(PARTS[parts[-1]])
         p = lax.dot_general(toks[g, lo:hi], wts[j], (((1,), (1,)), ((), ())), preferred_element_type=F32)
         p = p.T.astype(BF)
-        if whole:
-            for part in parts:
-                at, n = PARTS[part]
-                piece = p[:, at - lo:at - lo + n]
-                here = local_whole(j, g, part)
-
-                @pl.when(here)
-                def _():
-                    arrived_w[j - WHOLE, tensor, :, 0:n] = piece
-
-                @pl.when(jnp.logical_not(here))
-                def _():
-                    outgoing[j, g, :, at:at + n] = piece
-                    e_copy(j, g, part).start()
-            return
         here = local(j, g)
 
         @pl.when(here)
@@ -221,23 +193,17 @@
             for part in parts:
                 y_copy(j, g, part).start()
 
-    def split(lo, hi):
-        mid = min(max(lo, WHOLE), hi)
-        return [(a, b, w) for a, b, w in ((lo, mid, False), (mid, hi, True)) if b > a]
-
     def items(lo, hi, g, parts=(0, 1)):
-        for a, b, whole in split(lo, hi):
-            def body(j, carry, whole=whole):
-                item(j, g, parts, whole)
-                return carry
-            lax.fori_loop(a, b, body, 0)
+        def body(j, carry):
+            item(j, g, parts)
+            return carry
+        lax.fori_loop(lo, hi, body, 0)
 
     def items_both(lo, hi):
-        for a, b, whole in split(lo, hi):
-            def body(i, carry, a=a, whole=whole):
-                item(a + i // 2, i % 2, (0, 1), whole)
-                return carry
-            lax.fori_loop(0, 2 * (b - a), body, 0)
+        def body(i, carry):
+            item(lo + i // 2, i % 2, (0, 1))
+            return carry
+        lax.fori_loop(0, 2 * (hi - lo), body, 0)
 
     def msg_copy(i):
         return remote(msg, msgs.at[dp % 4], m_send.at[i], m_recv.at[dp % 4], (dp + i) % 32, tensor)
@@ -397,48 +363,11 @@
                 turned[j, ct] = part
                 x_copy(j, g, ct).start()
 
-    def f_copy(j, g, ct, part):
-        zs = zsrc_of(j)
-        tok_hi = jnp.where(g == 0, x_hi, 1 - x_hi)
-        src, dst = ((turned_a, whole_a), (turned_b, whole_b))[part]
-        return remote(src.at[j - WHOLE, ct], dst.at[zs % 2, core], f_send.at[j, ct],
-                      f_recv.at[zs % 2, core, part], dp_of(tok_hi, z, ct), x_hi * 4 + zs // 2)
-
-    def stage_whole(j, g):
-        for part in range(2):
-            @pl.when(share_lo(g, part) == x_lo)
-            def _(part=part):
-                n = PARTS[part][1]
-                for k in range(1, 8):
-                    frm = (tensor + k) % 8
-                    remote(outgoing.at[0, 0, :, pl.ds(0, n)], arrived_w.at[j - WHOLE, frm, :, pl.ds(0, n)],
-                           y_send.at[0, 0, part], e_recv.at[j, frm], dp, tensor).wait_recv()
-                total = arrived_w[j - WHOLE, 0, :, 0:n].astype(F32)
-                for k in range(1, 8):
-                    total = total + arrived_w[j - WHOLE, k, :, 0:n].astype(F32)
-                total = total.astype(BF)
-                src, dst = ((turned_a, whole_a), (turned_b, whole_b))[part]
-                for ct in range(2):
-                    piece = total[:, ct * (n // 2):(ct + 1) * (n // 2)]
-                    mine_too = to_self(j, g, ct)
-
-                    @pl.when(mine_too)
-                    def _():
-                        dst[zsrc_of(j) % 2, core] = piece
-
-                    @pl.when(jnp.logical_not(mine_too))
-                    def _():
-                        src[j - WHOLE, ct] = piece
-                        f_copy(j, g, ct, part).start()
-
     def second(lo, hi, g):
-        for a, b, whole in split(lo, hi):
-            stage = stage_whole if whole else stage_two
-
-            def unit(j, carry, stage=stage):
-                pl.when(active(j, g))(lambda: stage(j, g))
-                return carry
-            lax.fori_loop(a, b, unit, 0)
+        def unit(j, carry):
+            pl.when(active(j, g))(lambda: stage_two(j, g))
+            return carry
+        lax.fori_loop(lo, hi, unit, 0)
 
     def steps_of(zp):
         away = (2 * y + zp - z + 8) % 8
@@ -516,38 +445,19 @@
     def finish(i, carry):
         zp = jnp.where(steps_of(0) <= steps_of(1), i, 1 - i)
         away = jnp.where(x_lo == x_hi, 0, 1)
-        whole = steps_of(zp) >= FAR
-
-        @pl.when(jnp.logical_not(whole))
-        def _():
-            for cs in range(2):
-                for xl in range(2):
-                    frm = summer_at(y, away, cs)
-                    own_part = jnp.logical_and(jnp.logical_and(x_lo == x_hi, xl == x_lo),
-                                               jnp.logical_and(frm == y, core == cs))
-
-                    @pl.when(jnp.logical_not(own_part))
-                    def _():
-                        remote(turned.at[0, 0], halves.at[xl, zp, cs], x_send.at[0, 0], x_recv.at[xl, zp, cs],
-                               dp, tensor).wait_recv()
-                flat[cs * COLS:(cs + 1) * COLS, :] = halves[0, zp, cs].astype(F32) + halves[1, zp, cs].astype(F32)
-
-        @pl.when(whole)
-        def _():
-            for cs in range(2):
-                for part in range(2):
-                    frm = summer_at(y, away, cs)
-                    own_part = jnp.logical_and(jnp.logical_and(x_lo == x_hi, (part + away) % 2 == x_lo),
-                                               jnp.logical_and(frm == y, core == cs))
-                    src, dst = ((turned_a, whole_a), (turned_b, whole_b))[part]
-
-                    @pl.when(jnp.logical_not(own_part))
-                    def _():
-                        remote(src.at[0, 0], dst.at[zp, cs], f_send.at[0, 0], f_recv.at[zp, cs, part],
-                               dp, tensor).wait_recv()
-                flat[cs * COLS:(cs + 1) * COLS, 0:FIRST] = whole_a[zp, cs].astype(F32)
-                flat[cs * COLS:(cs + 1) * COLS, FIRST:TOK] = whole_b[zp, cs].astype(F32)
-        pre = extra[zp] + flat[...].T
+        parts = []
+        for cs in range(2):
+            for xl in range(2):
+                frm = summer_at(y, away, cs)
+                own_part = jnp.logical_and(jnp.logical_and(x_lo == x_hi, xl == x_lo),
+                                           jnp.logical_and(frm == y, core == cs))
+
+                @pl.when(jnp.logical_not(own_part))
+                def _():
+                    remote(turned.at[0, 0], halves.at[xl, zp, cs], x_send.at[0, 0], x_recv.at[xl, zp, cs],
+                           dp, tensor).wait_recv()
+            parts.append(halves[0, zp, cs].astype(F32) + halves[1, zp, cs].astype(F32))
+        pre = extra[zp] + jnp.concatenate(parts, axis=0).T
         sums[zp] = jnp.sum(cots[zp] * pre, axis=0, keepdims=True) / norms[zp]
         results[zp] = pre * scales[zp]
         return carry
@@ -611,20 +521,7 @@
                 def _():
                     x_copy(j, g, ct).wait_send()
         return carry
-    lax.fori_loop(0, WHOLE, drain, 0)
-
-    def drain_whole(j, carry):
-        for g in range(2):
-            for part in range(2):
-                @pl.when(jnp.logical_not(local_whole(j, g, part)))
-                def _():
-                    e_copy(j, g, part).wait_send()
-                for ct in range(2):
-                    @pl.when(jnp.logical_and(local_whole(j, g, part), jnp.logical_not(to_self(j, g, ct))))
-                    def _():
-                        f_copy(j, g, ct, part).wait_send()
-        return carry
-    lax.fori_loop(WHOLE, 8, drain_whole, 0)
+    lax.fori_loop(0, 8, drain, 0)
 
     def mag_arrive(i, total):
         frm = (dp + i) % 32
@@ -654,8 +551,8 @@
             vmem((2, 2 * TOK, HID), BF),
             vmem((8, COLS, HID), BF),
             vmem((8, 2, COLS, 2 * TOK), BF),
-            vmem((WHOLE, 4, COLS, 2 * TOK), BF),
-            vmem((WHOLE, 2, COLS, TOK), BF),
+            vmem((8, 4, COLS, 2 * TOK), BF),
+            vmem((8, 2, COLS, TOK), BF),
             vmem((2, 2, 2, COLS, TOK), BF),
             vmem((8, COLS), F32), vmem((8, 8, COLS), F32),
             vmem((16, 256), F32), vmem((16, 256), BF), vmem((4, 16, 256), BF),
@@ -669,13 +566,10 @@
             dma((8, 2, 2)), dma((8, 4, 2)), dma((8, 2)), dma((2, 2, 2)),
             dma((1,)), dma((8,)), dma((32,)), dma((4,)), dma((8,)), dma((8,)), dma((8,)), dma((8,)),
             dma((4,)), dma((4,)), dma((8,)), dma((8,)), dma((32,)), dma((32,)),
-            vmem((max(8 - WHOLE, 1), 8, COLS, 2 * FIRST), BF),
-            vmem((max(8 - WHOLE, 1), 2, COLS, FIRST), BF), vmem((max(8 - WHOLE, 1), 2, COLS, LAST), BF),
-            vmem((2, 2, COLS, FIRST), BF), vmem((2, 2, COLS, LAST), BF), vmem((2 * COLS, TOK), F32),
-            dma((8, 8)), dma((8, 2)), dma((2, 2, 2)), pltpu.SemaphoreType.REGULAR((3,)),
+            pltpu.SemaphoreType.REGULAR((3,)),
         ],
         compiler_params=pltpu.CompilerParams(
-            collective_id=0, has_side_effects=True, vmem_limit_bytes=67043328
+            collective_id=0, has_side_effects=True, vmem_limit_bytes=55779328
         ),
     )(hidden, weight.T, factor_b.T, factor_a, magnitude, cotangent)
     return mixed, gmag[0, :18], grads[:, 72:90], grads[:, :72].T

time: 109 us -> 106 us (0.972)
    pallas_call x1, Pallas kernels: 102 us -> 101 us  [body(): pl.pallas_call(kernel, name='dora', out_shape=(jax.ShapeDtypeStruct((TOK,...]
    unnamed x1 -> x7, local copies, waits for them, and re-layouts: 1.79 us -> 3.01 us
where the time goes in v6:
time: 106 us
  Pallas kernels  101 us (95%)
  local copies, waits for them, and re-layouts  4.79 us (5%)
    pallas_call x1, Pallas kernels, body(): pl.pallas_call(kernel, name='dora', out_shape=(jax.ShapeDtypeStruct((TOK,...  101 us
    unnamed x7, local copies, waits for them, and re-layouts  3.01 us

profile of v6, /device:TPU:1, one launch (start us, length us, event | category | flops | bytes accessed | tf_op | source)
XLA Modules:
  0.0 106.0 jit_solution(6497830799678596792)
XLA Ops:
  0.6 0.0 copy-start
  0.6 0.9 copy-done
  1.5 0.0 copy-start.1
  1.5 0.7 copy-done.1
  2.2 0.0 copy-start.2
  2.2 0.7 copy-done.2
  2.9 100.5 %dora.1 = (bf16[320,576]{1,0:T(8,128)(2,1)S(1)}, f32[16,128]{1,0:T(8,128)S(1)}, f32[1,128]{1,0:T(1,128)S(1)}) custom-call(bf16[320,2304]{1,0:T(8,128)(2,1)} %h_ref.1, bf16[144,2304]{1,0:T(8,128)(2,1)} %bitcast.7, bf16[16,2304]{1,0:T(8,128)(2,1)S(1)} %bitcast.6, bf16[16,144]{1,0:T(8,128)(2,1)S(1)} %copy-done.1, f32[576]{0:T(1024)S(1)} %copy-done.2, ...), custom_call_target="tpu_custom_call" | custom-call | tf_op jit(solution)/shard_map/dora/pallas_call | solution.py:542
  103.4 0.5 slice_bitcast_fusion.1
  103.9 0.6 slice_bitcast_fusion
  104.5 0.7 slice.10
  105.2 0.8 copy.11
Async XLA Ops:
  0.6 0.9 copy-start
  1.5 0.7 copy-start.1
  2.2 0.7 copy-start.2

commit v7 on v6

--- a/solution.py
+++ b/solution.py
@@ -424,13 +424,13 @@
         ring(3, 1)
     with jax.named_scope("b2_items"):
         items_both(5, 7)
+    with jax.named_scope("b3_second"):
+        second(3, 5, 0)
     with jax.named_scope("b5_last"):
         w_copy(0, 4, 0).wait_recv()
         w_copy(1, 4, 1).wait_recv()
     with jax.named_scope("b6_items"):
         items_both(7, 8)
-    with jax.named_scope("b7_second"):
-        second(3, 5, 0)
     with jax.named_scope("b8_grads"):
         gradients()
     with jax.named_scope("b9_second"):

time: 106 us -> 104 us (0.981)
  Pallas kernels: 101 us -> 98.8 us
    pallas_call x1, Pallas kernels: 101 us -> 98.8 us  [body(): pl.pallas_call(kernel, name='dora', out_shape=(jax.ShapeDtypeStruct((TOK,...]
where the time goes in v7:
time: 104 us
  Pallas kernels  98.8 us (95%)
  local copies, waits for them, and re-layouts  4.79 us (5%)
    pallas_call x1, Pallas kernels, body(): pl.pallas_call(kernel, name='dora', out_shape=(jax.ShapeDtypeStruct((TOK,...  98.8 us
    unnamed x7, local copies, waits for them, and re-layouts  3.01 us

profile of v7, /device:TPU:1, one launch (start us, length us, event | category | flops | bytes accessed | tf_op | source)
XLA Modules:
  0.0 104.3 jit_solution(9497188760270680829)
XLA Ops:
  0.6 0.0 copy-start
  0.6 0.9 copy-done
  1.5 0.0 copy-start.1
  1.5 0.7 copy-done.1
  2.2 0.0 copy-start.2
  2.2 0.7 copy-done.2
  2.9 98.8 %dora.1 = (bf16[320,576]{1,0:T(8,128)(2,1)S(1)}, f32[16,128]{1,0:T(8,128)S(1)}, f32[1,128]{1,0:T(1,128)S(1)}) custom-call(bf16[320,2304]{1,0:T(8,128)(2,1)} %h_ref.1, bf16[144,2304]{1,0:T(8,128)(2,1)} %bitcast.7, bf16[16,2304]{1,0:T(8,128)(2,1)S(1)} %bitcast.6, bf16[16,144]{1,0:T(8,128)(2,1)S(1)} %copy-done.1, f32[576]{0:T(1024)S(1)} %copy-done.2, ...), custom_call_target="tpu_custom_call" | custom-call | tf_op jit(solution)/shard_map/dora/pallas_call | solution.py:542
  101.7 0.5 slice_bitcast_fusion.1
  102.3 0.6 slice_bitcast_fusion
  102.9 0.7 slice.10
  103.5 0.8 copy.11
Async XLA Ops:
  0.6 0.9 copy-start
  1.5 0.7 copy-start.1
  2.2 0.7 copy-start.2

commit v8 on v7

--- a/solution.py
+++ b/solution.py
@@ -403,6 +403,8 @@
     with jax.named_scope("a6_relay0"):
         relay[0].wait_recv()
     items(0, 3, 1, (0,))
+    with jax.named_scope("aa_second"):
+        second(0, 3, 0)
     with jax.named_scope("a8_ring21"):
         ring(2, 1)
     items(3, 5, 0)
@@ -413,19 +415,17 @@
     with jax.named_scope("aa_receive"):
         receive()
     backward()
-    with jax.named_scope("aa_second"):
-        second(0, 3, 0)
     with jax.named_scope("ab_relay1"):
         relay[1].wait_recv()
     items(0, 5, 1, (1,))
     with jax.named_scope("ac_ring30"):
         ring(3, 0)
+    with jax.named_scope("b3_second"):
+        second(3, 5, 0)
     with jax.named_scope("b1_ring31"):
         ring(3, 1)
     with jax.named_scope("b2_items"):
         items_both(5, 7)
-    with jax.named_scope("b3_second"):
-        second(3, 5, 0)
     with jax.named_scope("b5_last"):
         w_copy(0, 4, 0).wait_recv()
         w_copy(1, 4, 1).wait_recv()

time: 104 us -> 109 us (1.048)
  Pallas kernels: 98.8 us -> 103 us
    pallas_call x1, Pallas kernels: 98.8 us -> 103 us  [body(): pl.pallas_call(kernel, name='dora', out_shape=(jax.ShapeDtypeStruct((TOK,...]
where the time goes in v8:
time: 109 us
  Pallas kernels  103 us (94%)
  local copies, waits for them, and re-layouts  4.79 us (4%)
    pallas_call x1, Pallas kernels, body(): pl.pallas_call(kernel, name='dora', out_shape=(jax.ShapeDtypeStruct((TOK,...  103 us
    unnamed x7, local copies, waits for them, and re-layouts  3.01 us

profile of v8, /device:TPU:1, one launch (start us, length us, event | category | flops | bytes accessed | tf_op | source)
XLA Modules:
  0.0 108.9 jit_solution(3913141467479775967)
XLA Ops:
  0.6 0.0 copy-start
  0.6 0.9 copy-done
  1.5 0.0 copy-start.1
  1.5 0.7 copy-done.1
  2.2 0.0 copy-start.2
  2.2 0.7 copy-done.2
  2.9 103.5 %dora.1 = (bf16[320,576]{1,0:T(8,128)(2,1)S(1)}, f32[16,128]{1,0:T(8,128)S(1)}, f32[1,128]{1,0:T(1,128)S(1)}) custom-call(bf16[320,2304]{1,0:T(8,128)(2,1)} %h_ref.1, bf16[144,2304]{1,0:T(8,128)(2,1)} %bitcast.7, bf16[16,2304]{1,0:T(8,128)(2,1)S(1)} %bitcast.6, bf16[16,144]{1,0:T(8,128)(2,1)S(1)} %copy-done.1, f32[576]{0:T(1024)S(1)} %copy-done.2, ...), custom_call_target="tpu_custom_call" | custom-call | tf_op jit(solution)/shard_map/dora/pallas_call | solution.py:542
  106.4 0.5 slice_bitcast_fusion.1
  106.9 0.6 slice_bitcast_fusion
  107.5 0.7 slice.10
  108.2 0.8 copy.11
Async XLA Ops:
  0.6 0.9 copy-start
  1.5 0.7 copy-start.1
  2.2 0.7 copy-start.2

commit v9 on v7

--- a/solution.py
+++ b/solution.py
@@ -11,7 +11,7 @@
 MESH = pl.DeviceIdType.MESH
 F32, BF = jnp.float32, jnp.bfloat16
 CHUNKS = ((0, 80), (80, 64))
-FIRST, LAST = 192, 128
+FIRST, LAST = 256, 64
 PARTS = ((0, 2 * FIRST), (2 * FIRST, 2 * LAST))
 
 
@@ -395,11 +395,11 @@
     with jax.named_scope("a3_ring11"):
         ring(1, 1)
     items(1, 3, 0)
+    with jax.named_scope("a5_ring20"):
+        ring(2, 0)
     with jax.named_scope("a4_far0"):
         to_far[0].wait_recv()
     relay[0].start()
-    with jax.named_scope("a5_ring20"):
-        ring(2, 0)
     with jax.named_scope("a6_relay0"):
         relay[0].wait_recv()
     items(0, 3, 1, (0,))

time: 104 us -> 111 us (1.067)
  Pallas kernels: 98.8 us -> 105 us
    pallas_call x1, Pallas kernels: 98.8 us -> 105 us  [body(): pl.pallas_call(kernel, name='dora', out_shape=(jax.ShapeDtypeStruct((TOK,...]
where the time goes in v9:
time: 111 us
  Pallas kernels  105 us (95%)
  local copies, waits for them, and re-layouts  4.79 us (4%)
    pallas_call x1, Pallas kernels, body(): pl.pallas_call(kernel, name='dora', out_shape=(jax.ShapeDtypeStruct((TOK,...  105 us
    unnamed x7, local copies, waits for them, and re-layouts  3.01 us

profile of v9, /device:TPU:1, one launch (start us, length us, event | category | flops | bytes accessed | tf_op | source)
XLA Modules:
  0.0 110.8 jit_solution(15160647798005704708)
XLA Ops:
  0.6 0.0 copy-start
  0.6 0.9 copy-done
  1.5 0.0 copy-start.1
  1.5 0.7 copy-done.1
  2.2 0.0 copy-start.2
  2.2 0.7 copy-done.2
  2.9 105.3 %dora.1 = (bf16[320,576]{1,0:T(8,128)(2,1)S(1)}, f32[16,128]{1,0:T(8,128)S(1)}, f32[1,128]{1,0:T(1,128)S(1)}) custom-call(bf16[320,2304]{1,0:T(8,128)(2,1)} %h_ref.1, bf16[144,2304]{1,0:T(8,128)(2,1)} %bitcast.7, bf16[16,2304]{1,0:T(8,128)(2,1)S(1)} %bitcast.6, bf16[16,144]{1,0:T(8,128)(2,1)S(1)} %copy-done.1, f32[576]{0:T(1024)S(1)} %copy-done.2, ...), custom_call_target="tpu_custom_call" | custom-call | tf_op jit(solution)/shard_map/dora/pallas_call | solution.py:542
  108.2 0.5 slice_bitcast_fusion.1
  108.8 0.6 slice_bitcast_fusion
  109.4 0.7 slice.10
  110.0 0.8 copy.11
Async XLA Ops:
  0.6 0.9 copy-start
  1.5 0.7 copy-start.1
  2.2 0.7 copy-start.2

commit v10 on v7

--- a/solution.py
+++ b/solution.py
@@ -431,13 +431,13 @@
         w_copy(1, 4, 1).wait_recv()
     with jax.named_scope("b6_items"):
         items_both(7, 8)
-    with jax.named_scope("b8_grads"):
-        gradients()
     with jax.named_scope("b9_second"):
         second(0, 5, 1)
     with jax.named_scope("ba_second"):
         second(5, 7, 0)
         second(5, 7, 1)
+    with jax.named_scope("b8_grads"):
+        gradients()
     with jax.named_scope("bb_second"):
         second(7, 8, 0)
         second(7, 8, 1)

time: 104 us -> 108 us (1.038)
  Pallas kernels: 98.8 us -> 103 us
    pallas_call x1, Pallas kernels: 98.8 us -> 103 us  [body(): pl.pallas_call(kernel, name='dora', out_shape=(jax.ShapeDtypeStruct((TOK,...]
where the time goes in v10:
time: 108 us
  Pallas kernels  103 us (95%)
  local copies, waits for them, and re-layouts  4.79 us (4%)
    pallas_call x1, Pallas kernels, body(): pl.pallas_call(kernel, name='dora', out_shape=(jax.ShapeDtypeStruct((TOK,...  103 us
    unnamed x7, local copies, waits for them, and re-layouts  3.01 us

profile of v10, /device:TPU:1, one launch (start us, length us, event | category | flops | bytes accessed | tf_op | source)
XLA Modules:
  0.0 108.0 jit_solution(17094367532617314762)
XLA Ops:
  0.6 0.0 copy-start
  0.6 0.9 copy-done
  1.5 0.0 copy-start.1
  1.5 0.7 copy-done.1
  2.2 0.0 copy-start.2
  2.2 0.7 copy-done.2
  2.9 102.5 %dora.1 = (bf16[320,576]{1,0:T(8,128)(2,1)S(1)}, f32[16,128]{1,0:T(8,128)S(1)}, f32[1,128]{1,0:T(1,128)S(1)}) custom-call(bf16[320,2304]{1,0:T(8,128)(2,1)} %h_ref.1, bf16[144,2304]{1,0:T(8,128)(2,1)} %bitcast.7, bf16[16,2304]{1,0:T(8,128)(2,1)S(1)} %bitcast.6, bf16[16,144]{1,0:T(8,128)(2,1)S(1)} %copy-done.1, f32[576]{0:T(1024)S(1)} %copy-done.2, ...), custom_call_target="tpu_custom_call" | custom-call | tf_op jit(solution)/shard_map/dora/pallas_call | solution.py:542
  105.4 0.5 slice_bitcast_fusion.1
  105.9 0.6 slice_bitcast_fusion
  106.5 0.7 slice.10
  107.2 0.8 copy.11
Async XLA Ops:
  0.6 0.9 copy-start
  1.5 0.7 copy-start.1
  2.2 0.7 copy-start.2
